TPU v7x, 32 devices: a whole 2x2x4 slice. The times are simulated.
32 devices in a mesh: dp: 8 (over z, core), tensor: 4 (over y, x).
Axes of the slice: x: 2, y: 2, z: 4, core: 2. Of those that a mesh axis runs over, the one named last changes fastest.
Arguments:
- hidden_in: bfloat16 [32, 128, 896], P('dp', 'tensor'), may hold values from -6 to 6
- targets: int32 [32, 128], P('dp', 'tensor'), may hold values from 0 to 98303
- doc_blocks: int32 [16], replicated, may hold values from 1 to 4, as said below
- ref_milli: int32 [16], replicated, may hold values from 8000 to 13999
- attn_gain: float32 [2, 896], replicated, may hold values from 0.3 to 3
- mlp_gain: float32 [2, 896], replicated, may hold values from 0.3 to 3
- final_gain: float32 [896], replicated, may hold values from 0.3 to 3
- w_query: bfloat16 [2, 896, 896], replicated, may hold values from -8.1 to 8.1
- w_key: bfloat16 [2, 896, 128], replicated, may hold values from -0.1875 to 0.1875
- w_value: bfloat16 [2, 896, 128], replicated, may hold values from -0.1875 to 0.1875
- w_out: bfloat16 [2, 896, 896], replicated, may hold values from -0.1875 to 0.1875
- w_gate: bfloat16 [2, 896, 4864], P(None, None, 'tensor'), may hold values from -0.1875 to 0.1875
- w_up: bfloat16 [2, 896, 4864], P(None, None, 'tensor'), may hold values from -0.1875 to 0.1875
- w_down: bfloat16 [2, 4864, 896], P(None, 'tensor'), may hold values from -0.078125 to 0.078125
- w_head: bfloat16 [896, 98304], P(None, ('dp', 'tensor')), may hold values from -41 to 41
Outputs:
- token_loss: float32 [32, 128], P('dp', 'tensor')
- scores: float32 [16], replicated
Inputs may be any that keep to these rules, and one draw needn't show every extreme that they name: `doc_blocks`: lengths of the documents in blocks, in pack order; they sum to 32.
All inputs are finite; a program needn't handle non-finite values.
Results may differ from a plain program's by a relative error of at most 0.035.
Values may be sent and summed in bfloat16 or wider, within the bound.
No kernel may reach another device: no remote copies, remote signals or barrier semaphores. Data moves between devices by JAX's collectives and lax.ppermute only.
A program may use at most 192 MiB of HBM per device.

v0:
```python
import math

import jax
import jax.numpy as jnp
from jax import lax
from jax.sharding import PartitionSpec as P

HEAD_DIM = 64
MAXB = 4


def from_behind(block, axis, distance):
    devices = range(lax.axis_size(axis))
    route = [(i - distance, i) for i in devices if i - distance in devices]
    return lax.ppermute(block, axis, route)


def doc_table(doc_blocks, nblk):
    ends = jnp.cumsum(doc_blocks)
    starts = ends - doc_blocks
    ids = jnp.arange(nblk, dtype=jnp.int32)
    owner = jnp.sum((starts[None, :] <= ids[:, None]).astype(jnp.int32), axis=1) - 1
    hit = owner[:, None] == jnp.arange(doc_blocks.shape[0], dtype=jnp.int32)[None, :]
    first = jnp.sum(jnp.where(hit, starts[None, :], 0), axis=1)
    return (owner, ids - first, first)


def lookup(block_ids, table, nblk):
    hit = block_ids[:, None] == jnp.arange(nblk, dtype=jnp.int32)[None, :]
    found = jnp.sum(jnp.where(hit, table[None, :], 0), axis=1)
    inside = (block_ids >= 0) & (block_ids < nblk)
    return (found, inside)


def norm_rows(h, gain):
    return h * lax.rsqrt(jnp.mean(h * h, axis=-1, keepdims=True) + 1e-06) * gain


def rotate(x, pos):
    half = x.shape[-1] // 2
    freq = jnp.exp(jnp.arange(half, dtype=jnp.float32) * (-2.0 * math.log(1000000.0) / x.shape[-1]))
    angle = pos.astype(jnp.float32)[..., None, None] * freq
    cosine = jnp.cos(angle)
    sine = jnp.sin(angle)
    first = x[..., :half]
    second = x[..., half:]
    return jnp.concatenate(
        [first * cosine - second * sine, second * cosine + first * sine], axis=-1
    )


def attend(query, keys, values, qdoc, qpos, kdoc, kpos):
    count, nheads, hdim = query.shape
    kvh = keys.shape[-1] // hdim
    q_five = query.reshape(count, kvh, nheads // kvh, hdim)
    k_three = keys.reshape(-1, kvh, hdim)
    v_three = values.reshape(-1, kvh, hdim)
    logits = jnp.einsum(
        "qcgd,kcd->cgqk", q_five, k_three, preferred_element_type=jnp.float32
    ) * hdim ** (-0.5)
    allowed = (
        (qdoc[:, None] == kdoc[None, :]) & (kpos[None, :] <= qpos[:, None]) & (kdoc[None, :] >= 0)
    )
    logits = jnp.where(allowed, logits, -1e30)
    peak = jnp.max(logits, axis=-1, keepdims=True)
    expo = jnp.exp(logits - peak)
    weights = (expo / jnp.sum(expo, axis=-1, keepdims=True)).astype(jnp.bfloat16)
    context = jnp.einsum("cgqk,kcd->qcgd", weights, v_three, preferred_element_type=jnp.float32)
    return context.reshape(count, nheads * hdim).astype(jnp.bfloat16)


def on_device(
    hidden_in,
    targets,
    doc_blocks,
    ref_milli,
    attn_gain,
    mlp_gain,
    final_gain,
    w_query,
    w_key,
    w_value,
    w_out,
    w_gate,
    w_up,
    w_down,
    w_head,
):
    dp_count = lax.axis_size("dp")
    tp_count = lax.axis_size("tensor")
    row = lax.axis_index("dp")
    column = lax.axis_index("tensor")
    own_blocks, slice_len, width = hidden_in.shape
    block_len = slice_len * tp_count
    nblk = own_blocks * dp_count
    ndoc = doc_blocks.shape[0]
    tails = MAXB - 1
    owner, offset, first = doc_table(doc_blocks, nblk)
    own_ids = row * own_blocks + jnp.arange(own_blocks, dtype=jnp.int32)
    slot_doc, live = lookup(own_ids, owner, nblk)
    slot_off, unused = lookup(own_ids, offset, nblk)
    prior_ids = row * own_blocks - tails + jnp.arange(tails, dtype=jnp.int32)
    prior_doc, prior_inside = lookup(prior_ids, owner, nblk)
    prior_off, unused = lookup(prior_ids, offset, nblk)
    key_doc_slots = jnp.concatenate([jnp.where(prior_inside, prior_doc, -1), slot_doc])
    key_off_slots = jnp.concatenate([prior_off, slot_off])
    slots = hidden_in.shape[0]
    query_pos = (
        slot_off[:, None] * block_len
        + column * slice_len
        + jnp.arange(slice_len, dtype=jnp.int32)[None, :]
    )
    query_doc = jnp.repeat(slot_doc, slice_len)
    key_doc = jnp.repeat(key_doc_slots, block_len)
    key_pos = (
        key_off_slots[:, None] * block_len + jnp.arange(block_len, dtype=jnp.int32)[None, :]
    ).reshape(-1)
    kv_width = w_key.shape[-1]
    heads = w_query.shape[-1] // HEAD_DIM
    h = hidden_in.astype(jnp.float32)
    for layer in range(w_query.shape[0]):
        normed = norm_rows(h, attn_gain[layer]).astype(jnp.bfloat16).reshape(-1, width)
        query = jnp.dot(normed, w_query[layer], preferred_element_type=jnp.float32).reshape(
            slots, slice_len, heads, HEAD_DIM
        )
        query = rotate(query, query_pos).astype(jnp.bfloat16).reshape(-1, heads, HEAD_DIM)
        keys = jnp.dot(normed, w_key[layer], preferred_element_type=jnp.float32).reshape(
            slots, slice_len, kv_width // HEAD_DIM, HEAD_DIM
        )
        keys = rotate(keys, query_pos).astype(jnp.bfloat16).reshape(slots, slice_len, kv_width)
        values = (
            jnp.dot(normed, w_value[layer], preferred_element_type=jnp.float32)
            .astype(jnp.bfloat16)
            .reshape(slots, slice_len, kv_width)
        )
        keys, values = (
            lax.all_gather(keys, "tensor", axis=1, tiled=True),
            lax.all_gather(values, "tensor", axis=1, tiled=True),
        )
        prior_keys, prior_values = from_behind((keys[-tails:], values[-tails:]), "dp", 1)
        keys = jnp.concatenate([prior_keys, keys], axis=0)
        values = jnp.concatenate([prior_values, values], axis=0)
        context = attend(
            query,
            keys.reshape(-1, kv_width),
            values.reshape(-1, kv_width),
            query_doc,
            query_pos.reshape(-1),
            key_doc,
            key_pos,
        )
        h = h + jnp.dot(context, w_out[layer], preferred_element_type=jnp.float32).reshape(h.shape)
        mixed = norm_rows(h, mlp_gain[layer]).astype(jnp.bfloat16)
        gate_layer = w_gate[layer]
        up_layer = w_up[layer]
        expand_piece = lax.all_gather(mixed, "tensor", axis=1, tiled=True)
        flat = expand_piece.reshape(-1, width)
        gate = jnp.dot(flat, gate_layer, preferred_element_type=jnp.float32)
        upper = jnp.dot(flat, up_layer, preferred_element_type=jnp.float32)
        middle = (
            (jax.nn.silu(gate) * upper)
            .astype(jnp.bfloat16)
            .reshape(expand_piece.shape[0], expand_piece.shape[1], gate_layer.shape[1])
        )
        partial_value = jnp.dot(
            middle.reshape(-1, middle.shape[-1]), w_down[layer], preferred_element_type=jnp.float32
        )
        h = h + lax.psum_scatter(
            partial_value.reshape(slots, block_len, width),
            "tensor",
            scatter_dimension=1,
            tiled=True,
        )
    final = norm_rows(h, final_gain).astype(jnp.bfloat16)
    rows_all, wanted_all = (
        lax.all_gather(final, "tensor", axis=1, tiled=True),
        lax.all_gather(targets, "tensor", axis=1, tiled=True),
    )
    rows_all = rows_all.reshape(-1, width)
    wanted_all = wanted_all.reshape(-1)
    vocab_shard = w_head.shape[1]
    count = rows_all.shape[0]
    piece = lax.all_gather(w_head, "dp", axis=1, tiled=True)
    top = jnp.full((count,), -1e30, jnp.float32)
    logits = jnp.dot(rows_all, piece, preferred_element_type=jnp.float32)
    cols = jnp.arange(piece.shape[1], dtype=jnp.int32)
    global_cols = (cols // vocab_shard * tp_count + column) * vocab_shard + cols % vocab_shard
    newtop = jnp.maximum(top, jnp.max(logits, axis=1))
    total = jnp.sum(jnp.exp(logits - newtop[:, None]), axis=1)
    picked = jnp.sum(jnp.where(global_cols[None, :] == wanted_all[:, None], logits, 0.0), axis=1)
    top, total, picked = (newtop, total, picked)
    peak = lax.pmax(top, "tensor")
    total, picked = lax.psum((total * jnp.exp(top - peak), picked), "tensor")
    row_loss = (jnp.log(total) + peak - picked).reshape(slots, block_len)
    own_loss = lax.dynamic_slice_in_dim(row_loss, column * slice_len, slice_len, 1)
    slot_sum = jnp.sum(own_loss, axis=1)
    hit = (slot_doc[:, None] == jnp.arange(ndoc, dtype=jnp.int32)[None, :]) & live[:, None]
    partial_docs = jnp.sum(jnp.where(hit, slot_sum[:, None], 0.0), axis=0)
    doc_total = lax.psum(partial_docs, ("dp", "tensor"))
    scores = ref_milli.astype(jnp.float32) * 0.001 - doc_total / (doc_blocks * block_len).astype(
        jnp.float32
    )
    return (own_loss, scores)


def solution(mesh):
    return jax.shard_map(
        on_device,
        mesh=mesh,
        in_specs=(
            P("dp", "tensor", None),
            P("dp", "tensor"),
            P(),
            P(),
            P(),
            P(),
            P(),
            P(),
            P(),
            P(),
            P(),
            P(None, None, "tensor"),
            P(None, None, "tensor"),
            P(None, "tensor", None),
            P(None, ("dp", "tensor")),
        ),
        out_specs=(P("dp", "tensor"), P()),
        check_vma=False,
    )
```

profile of v0, /device:TPU:0, one launch (start us, length us, event | category | flops | bytes accessed | tf_op | source)
XLA Modules:
  0.0 692.2 jit_solution(10679613952189118925)
XLA Ops:
  16.0 9.9 %all_gather.28 = bf16[4,128,128]{2,1,0:T(8,128)(2,1)S(1)} all-gather(bf16[4,32,128]{2,1,0:T(8,128)(2,1)S(1)} %convert_element_type.94), channel_id=1, replica_groups=mesh['dp'=8,'tensor'=4] {'tensor'}, dimensions={1}, use_global_device_ids=true | all-gather | bytes 163840 | tf_op jit(solution)/shard_map/all_gather | solution.py:137
  28.8 8.6 %all_gather.27 = bf16[4,128,128]{2,0,1:T(4,128)(2,1)S(1)} all-gather(bf16[4,32,128]{2,0,1:T(4,128)(2,1)S(1)} %copy.76), channel_id=1, replica_groups=mesh['dp'=8,'tensor'=4] {'tensor'}, dimensions={1}, use_global_device_ids=true | all-gather | bytes 163840 | tf_op jit(solution)/shard_map/all_gather | solution.py:138
  38.1 2.5 collective-permute-start
  41.3 2.2 slice_bitcast_fusion
  43.5 2.3 copy.82
  45.9 2.4 fusion.76
  55.2 4.8 fusion.117
  60.0 3.5 fusion.54
  67.2 13.8 %all_gather.29 = bf16[4,128,896]{2,1,0:T(8,128)(2,1)S(1)} all-gather(bf16[4,32,896]{2,1,0:T(8,128)(2,1)S(1)} %multiply_convert_fusion.3), channel_id=1, replica_groups=mesh['dp'=8,'tensor'=4] {'tensor'}, dimensions={1}, use_global_device_ids=true | all-gather | bytes 1146880 | tf_op jit(solution)/shard_map/all_gather | solution.py:156
  81.0 3.3 fusion.22
  84.3 3.5 fusion.39
  87.8 2.8 fusion.19
  94.1 28.3 %reduce-scatter.3.cloned.1.call-done = f32[4,32,896]{2,1,0:T(8,128)} async-done(((f32[4,128,896]{2,1,0:T(8,128)}), f32[4,32,896]{2,1,0:T(8,128)}) %reduce-scatter.3.cloned.1.call-update) | async-done | bytes 458768 | tf_op jit(solution)/shard_map/reduce_scatter | solution.py:168
  125.0 8.5 %all_gather.30 = bf16[4,128,128]{2,0,1:T(4,128)(2,1)S(1)} all-gather(bf16[4,32,128]{2,0,1:T(4,128)(2,1)S(1)} %copy.88), channel_id=1, replica_groups=mesh['dp'=8,'tensor'=4] {'tensor'}, dimensions={1}, use_global_device_ids=true | all-gather | bytes 163840 | tf_op jit(solution)/shard_map/all_gather | solution.py:138
  139.4 7.5 %all_gather.31 = bf16[4,128,128]{2,1,0:T(8,128)(2,1)S(1)} all-gather(bf16[4,32,128]{2,1,0:T(8,128)(2,1)S(1)} %convert_element_type.103), channel_id=1, replica_groups=mesh['dp'=8,'tensor'=4] {'tensor'}, dimensions={1}, use_global_device_ids=true | all-gather | bytes 163840 | tf_op jit(solution)/shard_map/all_gather | solution.py:137
  146.8 2.0 collective-permute-start.3
  150.9 4.8 fusion.122
  155.7 3.5 fusion.55
  160.0 1.9 multiply_reduce_fusion.1
  162.1 14.4 %all_gather.32 = bf16[4,128,896]{2,1,0:T(8,128)(2,1)S(1)} all-gather(bf16[4,32,896]{2,1,0:T(8,128)(2,1)S(1)} %multiply_convert_fusion.1), channel_id=1, replica_groups=mesh['dp'=8,'tensor'=4] {'tensor'}, dimensions={1}, use_global_device_ids=true | all-gather | bytes 1146880 | tf_op jit(solution)/shard_map/all_gather | solution.py:156
  176.5 3.3 fusion.17
  179.8 3.5 fusion.36
  183.3 2.8 fusion.14
  186.9 7.1 %all-gather = s32[4,32,4]{1,2,0:T(4,128)S(1)} all-gather(s32[1,32,4]{1,2,0:T(4,128)S(1)} %bitcast.223), channel_id=1, replica_groups=mesh['dp'=8,'tensor'=4] {'tensor'}, dimensions={0}, use_global_device_ids=true | all-gather | bytes 2560 | tf_op jit(solution)/shard_map/all_gather | solution.py:177
  194.1 25.8 %reduce-scatter.5.cloned.1.call-done = f32[4,32,896]{2,1,0:T(8,128)} async-done(((f32[4,128,896]{2,1,0:T(8,128)}), f32[4,32,896]{2,1,0:T(8,128)}) %reduce-scatter.5.cloned.1.call-update) | async-done | bytes 458768 | tf_op jit(solution)/shard_map/reduce_scatter | solution.py:168
  221.3 12.5 %all_gather.33 = bf16[4,128,896]{2,1,0:T(8,128)(2,1)S(1)} all-gather(bf16[4,32,896]{2,1,0:T(8,128)(2,1)S(1)} %multiply_convert_fusion), channel_id=1, replica_groups=mesh['dp'=8,'tensor'=4] {'tensor'}, dimensions={1}, use_global_device_ids=true | all-gather | bytes 1146880 | tf_op jit(solution)/shard_map/all_gather | solution.py:176
  233.8 331.1 %all-gather.3.cloned.1.call-done = bf16[896,24576]{1,0:T(8,128)(2,1)} async-done(((bf16[896,3072]{1,0:T(8,128)(2,1)}), bf16[896,24576]{1,0:T(8,128)(2,1)}) %all-gather.3.cloned.1.call-update) | async-done | bytes 44040208 | tf_op jit(solution)/shard_map/all_gather | solution.py:183
  564.8 39.9 %fusion.127 = (f32[512]{0:T(512)S(1)}, f32[512,24576]{1,0:T(8,128)}) fusion(bf16[512,896]{1,0:T(8,128)(2,1)S(1)} %bitcast.215, bf16[896,24576]{1,0:T(8,128)(2,1)} %all-gather.3.cloned.1.call-done), kind=kOutput, calls=%fused_computation.186 | convolution fusion | flops 22561161216 | bytes 95291392 | tf_op jit(solution)/shard_map/dot_general | solution.py:185
  604.7 9.8 %pmax.7 = f32[512]{0:T(512)S(1)} all-reduce(f32[512]{0:T(512)S(1)} %broadcast_maximum_fusion), channel_id=1, replica_groups=mesh['dp'=8,'tensor'=4] {'tensor'}, use_global_device_ids=true, to_apply=%region_20.21 | all-reduce | flops 512 | bytes 4096 | tf_op jit(solution)/shard_map/pmax | solution.py:192
  614.5 23.1 %exponential_reduce_fusion = (f32[512]{0:T(512)S(1)}, f32[512]{0:T(512)S(1)}) fusion(f32[512,24576]{1,0:T(8,128)} %get-tuple-element.45, f32[512]{0:T(512)S(1)} %broadcast_maximum_fusion, s32[512]{0:T(512)S(1)} %bitcast.222, s32[24576]{0:T(1024)S(1)} %fusion.100), kind=kLoop, calls=%fused_computation.3 | loop fusion | flops 62913536 | bytes 50438144 | tf_op jit(solution)/shard_map/reduce_sum | solution.py:189
  637.6 8.0 %all-reduce = (f32[512]{0:T(512)S(1)}, f32[512]{0:T(512)S(1)}) all-reduce(f32[512]{0:T(512)S(1)} %get-tuple-element.3, f32[512]{0:T(512)S(1)} %exponential_multiply_fusion), channel_id=1, replica_groups=mesh['dp'=8,'tensor'=4] {'tensor'}, use_global_device_ids=true, to_apply=%region_23.24 | all-reduce | flops 1024 | bytes 8192 | tf_op jit(solution)/shard_map/psum | solution.py:193
  646.5 37.8 %psum.23 = f32[16]{0:T(128)S(1)} all-reduce(f32[16]{0:T(128)S(1)} %select_reduce_fusion.2), channel_id=1, replica_groups=mesh['dp'=8,'tensor'=4] {'dp','tensor'}, use_global_device_ids=true, to_apply=%region_26.27 | all-reduce | flops 16 | bytes 128 | tf_op jit(solution)/shard_map/psum | solution.py:199
  (158 shorter events, 40.8 us)
Async XLA Ops:
  8.0 20.5 %copy-start.9 = (bf16[2,896,128]{2,1,0:T(8,128)(2,1)S(1)}, bf16[2,896,128]{2,1,0:T(8,128)(2,1)}, u32[]{:S(2)}) copy-start(bf16[2,896,128]{2,1,0:T(8,128)(2,1)} %param.24) | copy-start | bytes 1376260
  8.0 114.4 %reduce-scatter.3.cloned.1.call-start = ((), (), s32[]{:S(2)}) async-start(), calls=%async_computation.2 | async-start | bytes 2293760 | tf_op jit(solution)/shard_map/reduce_scatter | solution.py:168
  14.2 27.0 %copy-start.1 = (f32[4,32,32]{2,1,0:T(8,128)}, f32[4,32,32]{2,1,0:T(8,128)S(1)}, u32[]{:S(2)}) copy-start(f32[4,32,32]{2,1,0:T(8,128)S(1)} %get-tuple-element.33) | copy-start | bytes 49156
  25.9 2.8 copy-start.5
  26.6 25.6 %collective-permute-start.1 = (bf16[3,128,128]{2,1,0:T(8,128)(2,1)}, bf16[3,128,128]{2,1,0:T(8,128)(2,1)}, u32[]{:S(2)}, u32[]{:S(2)}) collective-permute-start(bf16[3,128,128]{2,1,0:T(8,128)(2,1)} %slice.123), channel_id=1, source_target_pairs={{0,4},{4,8},{8,12},{12,16},{16,20},{20,24},{24,28},{1,5},{5,9},{9,... | collective-permute-start | bytes 294920 | tf_op jit(solution)/shard_map/ppermute | solution.py:15
  37.4 3.9 copy-start.3
  38.1 15.5 %collective-permute-start = (bf16[3,128,128]{2,0,1:T(4,128)(2,1)}, bf16[3,128,128]{2,0,1:T(4,128)(2,1)}, u32[]{:S(2)}, u32[]{:S(2)}) collective-permute-start(bf16[3,128,128]{2,0,1:T(4,128)(2,1)} %slice.120), channel_id=1, source_target_pairs={{0,4},{4,8},{8,12},{12,16},{16,20},{20,24},{24,28},{1,5},{5,9},{9,... | collective-permute-start | bytes 294920 | tf_op jit(solution)/shard_map/ppermute | solution.py:15
  48.3 3.9 copy-start.13
  48.3 3.9 copy-start.6
  48.3 5.3 copy-start.4
  50.8 4.4 copy-start.12
  52.2 7.9 %copy-start.10 = (pred[128,896]{0,1:T(8,128)(4,1)}, pred[128,896]{0,1:T(8,128)(4,1)S(1)}, u32[]{:S(2)}) copy-start(pred[128,896]{0,1:T(8,128)(4,1)S(1)} %and_and_fusion) | copy-start | bytes 344068
  60.0 4.3 copy-start.7
  66.3 0.8 copy-start
  81.0 6.8 slice-start
  84.3 3.5 slice-start.1
  90.7 129.3 %reduce-scatter.5.cloned.1.call-start = ((), (), s32[]{:S(2)}) async-start(), calls=%async_computation.3 | async-start | bytes 2293760 | tf_op jit(solution)/shard_map/reduce_scatter | solution.py:168
  92.3 44.9 %copy-start.2 = (f32[4,32,32]{2,1,0:T(8,128)S(1)}, f32[4,32,32]{2,1,0:T(8,128)}, u32[]{:S(2)}) copy-start(f32[4,32,32]{2,1,0:T(8,128)} %copy-done.1) | copy-start | bytes 49156
  134.2 14.6 %collective-permute-start.2 = (bf16[3,128,128]{2,0,1:T(4,128)(2,1)}, bf16[3,128,128]{2,0,1:T(4,128)(2,1)}, u32[]{:S(2)}, u32[]{:S(2)}) collective-permute-start(bf16[3,128,128]{2,0,1:T(4,128)(2,1)} %slice.126), channel_id=1, source_target_pairs={{0,4},{4,8},{8,12},{12,16},{16,20},{20,24},{24,28},{1,5},{5,9},{9,... | collective-permute-start | bytes 294920 | tf_op jit(solution)/shard_map/ppermute | solution.py:15
  137.2 1.5 copy-start.8
  138.2 12.8 %copy-start.11 = (pred[128,896]{0,1:T(8,128)(4,1)S(1)}, pred[128,896]{0,1:T(8,128)(4,1)}, u32[]{:S(2)}) copy-start(pred[128,896]{0,1:T(8,128)(4,1)} %copy-done.10) | copy-start | bytes 344068
  146.8 3.6 collective-permute-start.3
  176.5 6.8 slice-start.2
  179.8 3.5 slice-start.3
  186.2 0.7 copy-start.15
  186.2 35.0 %copy-start.14 = (f32[896]{0:T(1024)S(1)}, f32[896]{0:T(1024)}, u32[]{:S(2)}) copy-start(f32[896]{0:T(1024)} %param.21) | copy-start | bytes 10756
  186.2 378.7 %all-gather.3.cloned.1.call-start = ((), (), s32[]{:S(2)}) async-start(), calls=%async_computation.4 | async-start | bytes 49545216 | tf_op jit(solution)/shard_map/all_gather | solution.py:183
  614.5 69.7 %copy-start.16 = (s32[16]{0:T(128)S(1)}, s32[16]{0:T(128)}, u32[]{:S(2)}) copy-start(s32[16]{0:T(128)} %param.17) | copy-start | bytes 196
  614.5 69.7 %copy-start.17 = (s32[16]{0:T(128)S(1)}, s32[16]{0:T(128)}, u32[]{:S(2)}) copy-start(s32[16]{0:T(128)} %param.18) | copy-start | bytes 196
Sparse Core Ops, SparseCore 0:
  90.8 31.5 reduce-scatter.2
  186.3 33.6 reduce-scatter.4
Sparse Core Ops, SparseCore 1:
  188.3 376.5 all-gather.2
where the time goes:
time: 693 us; the launch traced here: 692 us
  waiting for transfers between devices  386 us (56%)
  blocking collectives  138 us (20%)
  matrix products  84.8 us (12%)
  other arithmetic  37.5 us (5%)
  local copies, waits for them, and re-layouts  21.5 us (3%)
  between operations  16.2 us (2%)
  starting transfers between devices  8.43 us (1%)
    all_gather x1, waiting for transfers between devices, on_device(): piece = lax.all_gather(w_head, 'dp', axis=1, tiled=True)  331 us
    reduce_scatter x2, waiting for transfers between devices, on_device(): lax.psum_scatter(partial_value.reshape(slots, block_len, width), 'tensor'...  54.1 us
    dot_general x1, matrix products, on_device(): logits = jnp.dot(rows_all, piece, preferred_element_type=jnp.float32)  39.9 us
    psum x1, blocking collectives, on_device(): doc_total = lax.psum(partial_docs, ('dp', 'tensor'))  37.8 us
    all_gather x2, blocking collectives, on_device(): expand_piece = lax.all_gather(mixed, 'tensor', axis=1, tiled=True)  28.2 us
    reduce_sum x1, other arithmetic, on_device(): total = jnp.sum(jnp.exp(logits - newtop[:, None]), axis=1)  23.1 us
    all_gather x2, blocking collectives, on_device(): lax.all_gather(keys, 'tensor', axis=1, tiled=True)  17.4 us
    all_gather x2, blocking collectives, on_device(): lax.all_gather(values, 'tensor', axis=1, tiled=True)  17.1 us
  transfers between devices with their start and end apart: 7, of which 3 were waited for; matrix products, arithmetic and copies ran while one was open for 3% of the time, Pallas kernels for 0%

commit v1 on v0

v1 whole, which is shorter than its diff:
```python
import math

import jax
import jax.numpy as jnp
from jax import lax
from jax.experimental import pallas as pl
from jax.experimental.pallas import tpu as pltpu
from jax.sharding import Mesh
from jax.sharding import PartitionSpec as P

HEAD_DIM = 64
MAXB = 4
LANES = 128
NEG = -1e30
BF16 = jnp.bfloat16
F32 = jnp.float32
DP = ("zp", "zq", "core")
ALL = ("zp", "zq", "core", "tensor")
MIB = 1024 * 1024


def doc_table(doc_blocks, nblk):
    ends = jnp.cumsum(doc_blocks)
    starts = ends - doc_blocks
    ids = jnp.arange(nblk, dtype=jnp.int32)
    owner = jnp.sum((starts[None, :] <= ids[:, None]).astype(jnp.int32), axis=1) - 1
    hit = owner[:, None] == jnp.arange(doc_blocks.shape[0], dtype=jnp.int32)[None, :]
    first = jnp.sum(jnp.where(hit, starts[None, :], 0), axis=1)
    return (owner, ids - first)


def lookup(block_ids, table, nblk):
    hit = block_ids[:, None] == jnp.arange(nblk, dtype=jnp.int32)[None, :]
    found = jnp.sum(jnp.where(hit, table[None, :], 0), axis=1)
    inside = (block_ids >= 0) & (block_ids < nblk)
    return (found, inside)


def norm_rows(h, gain):
    scaled = h * lax.rsqrt(jnp.mean(h * h, axis=-1, keepdims=True) + 1e-06)
    return (scaled.reshape(-1, 8, h.shape[1]) * gain[None]).reshape(h.shape)


def tall(gain):
    shape = gain.shape[:-1] + (8, gain.shape[-1])
    return jnp.broadcast_to(gain[..., None, :], shape)


def dot(x, y):
    return jnp.dot(x, y, preferred_element_type=F32)


def dot_t(x, y):
    return lax.dot_general(x, y, (((1,), (1,)), ((), ())), preferred_element_type=F32)


def whole(shape):
    return pl.BlockSpec(shape, lambda *_: (0,) * len(shape))


def layer_of(array, layer):
    shape = array.shape[1:]
    return pl.BlockSpec((None,) + shape, lambda *_: (layer,) + (0,) * len(shape))


def cost(flops, moved):
    return pl.CostEstimate(flops=int(flops), bytes_accessed=int(moved), transcendentals=0)


def params(mib):
    return pltpu.CompilerParams(vmem_limit_bytes=mib * MIB)


def rotate_lanes(x, cosine, sine):
    lane = lax.broadcasted_iota(jnp.int32, (x.shape[0], LANES), 1)
    lower = lane % HEAD_DIM < HEAD_DIM // 2
    pieces = []
    for at in range(0, x.shape[1], LANES):
        part = x[:, at : at + LANES]
        other = jnp.where(
            lower,
            pltpu.roll(part, LANES - HEAD_DIM // 2, 1),
            pltpu.roll(part, HEAD_DIM // 2, 1),
        )
        pieces.append(part * cosine + other * sine)
    return pieces


def add_parts(h, refs):
    for ref in refs:
        h = h + ref[...].astype(F32)
    return h


def key_value(h, parts, gains, w_key, w_value, cosine, sine, layer):
    count, width = h.shape
    kvw = w_key.shape[-1]

    def body(*refs):
        h_ref, given, refs = refs[0], refs[1 : 1 + len(parts)], refs[1 + len(parts) :]
        value = add_parts(h_ref[...].astype(F32), given)
        gain_ref, wk_ref, wv_ref, cos_ref, sin_ref, h_out, a_out, kv_out = refs
        h_out[...] = value
        a = norm_rows(value, gain_ref[...]).astype(BF16)
        a_out[...] = a
        keys = rotate_lanes(dot(a, wk_ref[...]), cos_ref[...], sin_ref[...])
        for at, piece in enumerate(keys):
            kv_out[:, at * LANES : (at + 1) * LANES] = piece.astype(BF16)
        kv_out[:, kvw:] = dot(a, wv_ref[...]).astype(BF16)

    args = [h] + parts + [gains, w_key, w_value, cosine, sine]
    specs = [whole(x.shape) for x in args]
    specs[-5] = layer_of(gains, layer)
    specs[-4] = layer_of(w_key, layer)
    specs[-3] = layer_of(w_value, layer)
    outs = (
        jax.ShapeDtypeStruct((count, width), F32),
        jax.ShapeDtypeStruct((count, width), BF16),
        jax.ShapeDtypeStruct((count, 2 * kvw), BF16),
    )
    return pl.pallas_call(
        body,
        grid=(1,),
        out_shape=outs,
        in_specs=specs,
        out_specs=[whole(o.shape) for o in outs],
        compiler_params=params(12),
        cost_estimate=cost(2.0 * count * width * 2 * kvw, 0),
        name="key_value",
    )(*args)


def queries(a, w_query, cosine, sine, layer):
    count = a.shape[0]
    out = w_query.shape[-1]

    def body(a_ref, w_ref, cos_ref, sin_ref, q_out):
        q = rotate_lanes(dot(a_ref[...], w_ref[...]), cos_ref[...], sin_ref[...])
        for at, piece in enumerate(q):
            q_out[:, at * LANES : (at + 1) * LANES] = piece.astype(BF16)

    shape = (count, out)
    return pl.pallas_call(
        body,
        grid=(1,),
        out_shape=jax.ShapeDtypeStruct(shape, BF16),
        in_specs=[
            whole(a.shape),
            layer_of(w_query, layer),
            whole(cosine.shape),
            whole(sine.shape),
        ],
        out_specs=whole(shape),
        compiler_params=params(10),
        cost_estimate=cost(2.0 * count * out * out, 0),
        name="queries",
    )(a, w_query, cosine, sine)


def attention(q, kv, bias, h, w_out, gains, layer):
    blocks, rows, span = bias.shape
    count, qw = q.shape
    width = h.shape[1]
    kvw = kv.shape[1] // 2
    kvh = kvw // HEAD_DIM
    heads = qw // HEAD_DIM
    group = heads // kvh
    pairs = heads // 2
    block_len = span // MAXB
    assert kvw == LANES and kvh == 2

    def body(q_ref, kv_ref, bias_ref, h_ref, wo_ref, gain_ref, h_out, b_out, score, ctx):
        low = lax.broadcasted_iota(jnp.int32, (kv_ref.shape[0], LANES), 1) < HEAD_DIM

        def variants(x, other):
            turned = pltpu.roll(x, HEAD_DIM, 1)
            return {
                (0, 0): jnp.where(low, x, other).astype(BF16),
                (1, 1): jnp.where(low, other, x).astype(BF16),
                (0, 1): jnp.where(low, turned, other).astype(BF16),
                (1, 0): jnp.where(low, other, turned).astype(BF16),
            }

        keys = variants(kv_ref[:, :kvw].astype(F32), 0.0)
        values = variants(kv_ref[:, kvw:].astype(F32), 1.0)
        work = []
        at = 0
        for i in range(blocks):
            for half in range(2):
                for c in range(kvh):
                    mine = [j for j in range(pairs) if (2 * j + half) // group == c]
                    if mine:
                        work.append((i, half, c, mine, at))
                        at += len(mine) * rows
        for i, half, c, mine, at in work:
            window = slice(i * block_len, i * block_len + span)
            stack = [q_ref[i * rows : (i + 1) * rows, j * LANES : (j + 1) * LANES] for j in mine]
            found = dot_t(jnp.concatenate(stack, axis=0), keys[(half, c)][window])
            for n in range(len(mine)):
                piece = found[n * rows : (n + 1) * rows] * HEAD_DIM ** (-0.5) + bias_ref[i]
                score[at + n * rows : at + (n + 1) * rows] = piece
        halves = {}
        for i, half, c, mine, at in work:
            window = slice(i * block_len, i * block_len + span)
            piece = score[at : at + len(mine) * rows]
            expo = jnp.exp(piece - jnp.max(piece, axis=-1, keepdims=True)).astype(BF16)
            got = dot(expo, values[(half, c)][window])
            got = got / pltpu.roll(got, HEAD_DIM, 1)
            for n, j in enumerate(mine):
                halves[(i, j, half)] = got[n * rows : (n + 1) * rows]
        first = low[:rows]
        for i in range(blocks):
            for j in range(pairs):
                ctx[i * rows : (i + 1) * rows, j * LANES : (j + 1) * LANES] = jnp.where(
                    first, halves[(i, j, 0)], halves[(i, j, 1)]
                )
        value = h_ref[...] + dot(ctx[...].astype(BF16), wo_ref[...])
        h_out[...] = value
        b_out[...] = norm_rows(value, gain_ref[...]).astype(BF16)

    args = (q, kv, bias, h, w_out, gains)
    specs = [whole(x.shape) for x in args]
    specs[4] = layer_of(w_out, layer)
    specs[5] = layer_of(gains, layer)
    outs = (
        jax.ShapeDtypeStruct((count, width), F32),
        jax.ShapeDtypeStruct((count, width), BF16),
    )
    return pl.pallas_call(
        body,
        grid=(1,),
        out_shape=outs,
        in_specs=specs,
        out_specs=[whole(o.shape) for o in outs],
        scratch_shapes=[
            pltpu.VMEM((blocks * heads * rows, span), F32),
            pltpu.VMEM((count, qw), F32),
        ],
        compiler_params=params(20),
        cost_estimate=cost(2.0 * count * width * width + 8.0 * count * qw * span, 0),
        name="attention",
    )(*args)


def mlp(x, w_gate, w_up, w_down, layer, kind):
    count, width = x.shape
    step = min(count, 256)

    def body(x_ref, wg_ref, wu_ref, wd_ref, out_ref):
        for at in range(0, count, step):
            rows = x_ref[at : at + step]
            gate = dot_t(rows, wg_ref[...])
            upper = dot_t(rows, wu_ref[...])
            middle = (gate / (1.0 + jnp.exp(-gate)) * upper).astype(BF16)
            out_ref[at : at + step] = dot(middle, wd_ref[...]).astype(kind)

    return pl.pallas_call(
        body,
        grid=(1,),
        out_shape=jax.ShapeDtypeStruct((count, width), kind),
        in_specs=[
            whole(x.shape),
            layer_of(w_gate, layer),
            layer_of(w_up, layer),
            layer_of(w_down, layer),
        ],
        out_specs=whole((count, width)),
        compiler_params=params(28),
        cost_estimate=cost(6.0 * count * width * w_down.shape[1], 0),
        name="mlp",
    )(x, w_gate, w_up, w_down)


def last_norm(h, parts, gain):
    def body(h_ref, *refs):
        gain_ref, out_ref = refs[-2:]
        value = add_parts(h_ref[...], refs[:-2])
        out_ref[...] = norm_rows(value, gain_ref[...]).astype(BF16)

    args = [h] + parts + [gain]
    return pl.pallas_call(
        body,
        grid=(1,),
        out_shape=jax.ShapeDtypeStruct(h.shape, BF16),
        in_specs=[whole(x.shape) for x in args],
        out_specs=whole(h.shape),
        compiler_params=params(8),
        name="last_norm",
    )(*args)


def head_stats(rows, wanted, bases, shards):
    count = sum(x.shape[0] for x in rows)
    width = rows[0].shape[1]
    cols = shards[0].shape[1]
    tile = next(t for t in (1024, 768, 512, 384, 256, 128) if cols % t == 0)
    chunk = tile // 2 if tile % 256 == 0 else tile
    per = cols // tile
    steps = per * len(shards)

    def body(base_ref, want_ref, *rest):
        given = rest[: len(rows)]
        w_refs = rest[len(rows) : len(rows) + len(shards)]
        out_ref, top, total, picked, wide, x_ref = rest[len(rows) + len(shards) :]
        step = pl.program_id(0)

        @pl.when(step == 0)
        def _():
            top[...] = jnp.full_like(top, NEG)
            total[...] = jnp.zeros_like(total)
            picked[...] = jnp.zeros_like(picked)
            wide[...] = jnp.broadcast_to(want_ref[...], wide.shape)
            at = 0
            for ref in given:
                x_ref[at : at + ref.shape[0]] = ref[...]
                at += ref.shape[0]

        lane = lax.broadcasted_iota(jnp.int32, (1, LANES), 1)

        def use(w_ref, index):
            start = base_ref[index] + (step - index * per) * tile
            local = wide[...]
            for at in range(0, tile, chunk):
                logits = dot(x_ref[...], w_ref[:, at : at + chunk])
                parts = [logits[:, c : c + LANES] for c in range(0, chunk, LANES)]
                best = parts[0]
                for part in parts[1:]:
                    best = jnp.maximum(best, part)
                old = top[...]
                best = jnp.maximum(best, old)
                acc = total[...] * jnp.exp(old - best)
                pick = picked[...]
                for n, part in enumerate(parts):
                    acc = acc + jnp.exp(part - best)
                    pick = pick + jnp.where(local == lane + (start + at + n * LANES), part, 0.0)
                top[...] = best
                total[...] = acc
                picked[...] = pick

        for index, w_ref in enumerate(w_refs):
            pl.when(step // per == index)(lambda r=w_ref, n=index: use(r, n))

        @pl.when(step == steps - 1)
        def _():
            best = jnp.max(top[...], axis=1, keepdims=True)
            acc = jnp.sum(total[...] * jnp.exp(top[...] - best), axis=1, keepdims=True)
            pick = jnp.sum(picked[...], axis=1, keepdims=True)
            packed = jnp.where(lane == 0, best, jnp.where(lane == 1, acc, pick))
            out_ref[...] = jnp.transpose(packed, (1, 0))[:8]

    def column_spec(index):
        return pl.BlockSpec((width, tile), lambda s: (0, jnp.clip(s - index * per, 0, per - 1)))

    return pl.pallas_call(
        body,
        grid=(steps,),
        out_shape=jax.ShapeDtypeStruct((8, count), F32),
        in_specs=[
            pl.BlockSpec(memory_space=pltpu.SMEM),
            whole(wanted.shape),
        ]
        + [whole(x.shape) for x in rows]
        + [column_spec(n) for n in range(len(shards))],
        out_specs=whole((8, count)),
        scratch_shapes=[pltpu.VMEM((count, LANES), F32)] * 3
        + [pltpu.VMEM((count, LANES), jnp.int32), pltpu.VMEM((count, width), BF16)],
        compiler_params=params(20),
        cost_estimate=cost(2.0 * count * width * cols * len(shards), 0),
        name="head_stats",
    )(bases, wanted, *rows, *shards)


def shift(x, axes, distance, size, wrap):
    pairs = [(i, (i + distance) % size) for i in range(size) if wrap or i + distance < size]
    return lax.ppermute(x, axes, pairs)


def on_device(
    hidden_in,
    targets,
    doc_blocks,
    ref_milli,
    attn_gain,
    mlp_gain,
    final_gain,
    w_query,
    w_key,
    w_value,
    w_out,
    w_gate,
    w_up,
    w_down,
    w_head,
):
    zp_count = lax.axis_size("zp")
    core_count = lax.axis_size("core")
    dp_count = lax.axis_size(DP)
    tp_count = lax.axis_size("tensor")
    device_count = dp_count * tp_count
    row = lax.axis_index(DP)
    column = lax.axis_index("tensor")
    own_blocks, slice_len, width = hidden_in.shape
    block_len = slice_len * tp_count
    nblk = own_blocks * dp_count
    ndoc = doc_blocks.shape[0]
    tails = MAXB - 1
    own_count = own_blocks * slice_len
    vocab_shard = w_head.shape[1]

    direct = tp_count in (2, 4)

    def peer(x, k):
        return lax.ppermute(x, "tensor", [(i, i ^ k) for i in range(tp_count)])

    if core_count > 1:
        swap = [(i, core_count - 1 - i) for i in range(core_count)]
        shards = [w_head, lax.ppermute(w_head, "core", swap)]
        holders = [row, row - 2 * lax.axis_index("core") + 1]
    else:
        shards = [w_head]
        holders = [row]
    bases = jnp.stack([(r * tp_count + column) * vocab_shard for r in holders]).astype(jnp.int32)
    ids = targets.reshape(1, own_count)
    digits = jnp.concatenate([ids // 16384, ids // 128 % 128, ids % 128], axis=0).astype(BF16)
    digits = jnp.pad(digits, ((0, slice_len - 3), (0, 4 * HEAD_DIM - own_count)))[None]

    owner, offset = doc_table(doc_blocks, nblk)
    own_ids = row * own_blocks + jnp.arange(own_blocks, dtype=jnp.int32)
    slot_doc, live = lookup(own_ids, owner, nblk)
    slot_off, unused = lookup(own_ids, offset, nblk)
    prior_ids = row * own_blocks - tails + jnp.arange(tails, dtype=jnp.int32)
    prior_doc, prior_inside = lookup(prior_ids, owner, nblk)
    key_doc = jnp.concatenate([jnp.where(prior_inside, prior_doc, -1), slot_doc])
    window_doc = jnp.stack([key_doc[i : i + MAXB] for i in range(own_blocks)])
    same = (window_doc == slot_doc[:, None]) & (window_doc >= 0)
    place = column * slice_len + jnp.arange(slice_len, dtype=jnp.int32)
    inner = jnp.arange(block_len, dtype=jnp.int32)
    causal = inner[None, :] <= place[:, None]
    slot = jnp.arange(MAXB, dtype=jnp.int32)
    seen = (slot[None, :, None] < tails) | causal[:, None, :]
    bias = jnp.where(same[:, None, :, None] & seen[None], 0.0, NEG).astype(F32)
    bias = bias.reshape(own_blocks, slice_len, MAXB * block_len)

    pos = (slot_off[:, None] * block_len + place[None, :]).reshape(-1).astype(F32)
    half = HEAD_DIM // 2
    lane = jnp.arange(LANES, dtype=jnp.int32)
    freq = jnp.exp((lane % half).astype(F32) * (-2.0 * math.log(1000000.0) / HEAD_DIM))
    angle = pos[:, None] * freq[None, :]
    cosine = jnp.cos(angle)
    sine = jnp.sin(angle) * jnp.where(lane % HEAD_DIM < half, -1.0, 1.0)[None, :]

    h = hidden_in.reshape(own_count, width)
    attn_gain = tall(attn_gain)
    mlp_gain = tall(mlp_gain)
    w_gate = w_gate.transpose(0, 2, 1)
    w_up = w_up.transpose(0, 2, 1)
    parts = []
    for layer in range(w_query.shape[0]):
        h, a, kv = key_value(h, parts, attn_gain, w_key, w_value, cosine, sine, layer)
        kvw = kv.shape[1]
        kv = kv.reshape(own_blocks, slice_len, kvw)
        tail = shift(kv[own_blocks - tails :], DP, 1, dp_count, False)
        q = queries(a, w_query, cosine, sine, layer)
        kv = jnp.concatenate([tail, kv] + ([digits] if layer == 0 else []), axis=0)
        kv = lax.all_gather(kv, "tensor", axis=1, tiled=True)
        if layer == 0:
            found = kv[-1].reshape(tp_count, slice_len, kvw)[:, :3, :own_count].astype(jnp.int32)
            wanted_row = found[:, 0] * 16384 + found[:, 1] * 128 + found[:, 2]
            kv = kv[:-1]
        h, b = attention(
            q,
            kv.reshape(-1, kvw),
            bias,
            h,
            w_out,
            mlp_gain,
            layer,
        )
        if direct:
            given = [b] + [peer(b, k) for k in range(1, tp_count)]
            kinds = [F32] + [BF16] * (tp_count - 1)
            parts = [mlp(x, w_gate, w_up, w_down, layer, t) for x, t in zip(given, kinds)]
            parts = parts[:1] + [peer(parts[k], k) for k in range(1, tp_count)]
        else:
            flat = lax.all_gather(b, "tensor", axis=0, tiled=True)
            out = mlp(flat, w_gate, w_up, w_down, layer, BF16)
            out = out.reshape(tp_count, own_count, width)
            out = lax.all_to_all(out, "tensor", 0, 0, tiled=False)
            parts = [out[k] for k in range(tp_count)]
    final = last_norm(h, parts, tall(final_gain))

    zq_count = lax.axis_size("zq")
    pieces = []
    for turn_q in range(zq_count):
        for turn in range(zp_count):
            rows, wanted = final, wanted_row
            if turn:
                rows = shift(rows, "zp", turn, zp_count, True)
                wanted = shift(wanted, "zp", turn, zp_count, True)
            if turn_q:
                rows = shift(rows, "zq", turn_q, zq_count, True)
                wanted = shift(wanted, "zq", turn_q, zq_count, True)
            pieces.append((rows, wanted))
    stats = []
    first = lax.all_gather(final, "tensor", axis=0, tiled=True)
    chunk, done = [first], first
    order = [column ^ k for k in range(tp_count)]
    for n in range(len(pieces)):
        wanted = pieces[n][1]
        if n and direct:
            wanted = [lax.dynamic_slice_in_dim(wanted, k, 1, 0) for k in order]
            wanted = jnp.concatenate(wanted, axis=0)
        following = None
        if n + 1 < len(pieces):
            rows, done = lax.optimization_barrier((pieces[n + 1][0], done))
            if direct:
                following = [rows] + [peer(rows, k) for k in range(1, tp_count)]
            else:
                following = [lax.all_gather(rows, "tensor", axis=0, tiled=True)]
        stats.append(head_stats(chunk, wanted.reshape(-1, 1), bases, shards))
        chunk, done = following, stats[-1]
    stats = jnp.stack(stats)
    stats = stats.reshape(zq_count, zp_count, 8, tp_count, own_count)
    if direct:
        mixed = [jnp.take(stats, column ^ jnp.arange(tp_count), axis=3)]
        plain = stats.reshape(-1, 8, tp_count, own_count)[:1]
        mixed = mixed[0].reshape(-1, 8, tp_count, own_count)[1:]
        stats = jnp.concatenate([plain, mixed]).reshape(stats.shape)
    zp_at = (lax.axis_index("zp") - jnp.arange(zp_count)) % zp_count
    zq_at = (lax.axis_index("zq") - jnp.arange(zq_count)) % zq_count
    stats = jnp.take(jnp.take(stats, zp_at, axis=1), zq_at, axis=0)
    stats = stats[:, :, :3].transpose(1, 0, 3, 2, 4)
    stats = stats.reshape(zp_count * zq_count * tp_count, 3, own_count)
    stats = lax.all_to_all(stats, ("zp", "zq", "tensor"), 0, 0, tiled=False)
    peak = jnp.max(stats[:, 0], axis=0)
    total = jnp.sum(stats[:, 1] * jnp.exp(stats[:, 0] - peak[None]), axis=0)
    own_loss = jnp.log(total) + peak - jnp.sum(stats[:, 2], axis=0)
    own_loss = own_loss.reshape(own_blocks, slice_len)

    slot_sum = jnp.sum(own_loss, axis=1)
    hit = (slot_doc[:, None] == jnp.arange(ndoc, dtype=jnp.int32)[None, :]) & live[:, None]
    partial_docs = jnp.sum(jnp.where(hit, slot_sum[:, None], 0.0), axis=0)
    padded = jnp.pad(partial_docs, (0, LANES - ndoc))
    spread = jnp.broadcast_to(padded[None], (device_count, LANES))
    doc_total = jnp.sum(lax.all_to_all(spread, ALL, 0, 0, tiled=False), axis=0)[:ndoc]
    scores = ref_milli.astype(F32) * 0.001 - doc_total / (doc_blocks * block_len).astype(F32)
    return (own_loss, scores)


def solution(mesh):
    dp_count, tp_count = mesh.shape["dp"], mesh.shape["tensor"]
    core = 2 if dp_count % 2 == 0 else 1
    depth = dp_count // core
    pair = 2 if depth % 2 == 0 else 1
    devices = mesh.devices.reshape(depth // pair, pair, core, tp_count)
    return jax.shard_map(
        on_device,
        mesh=Mesh(devices, ALL),
        in_specs=(
            P(DP, "tensor", None),
            P(DP, "tensor"),
            P(),
            P(),
            P(),
            P(),
            P(),
            P(),
            P(),
            P(),
            P(),
            P(None, None, "tensor"),
            P(None, None, "tensor"),
            P(None, "tensor", None),
            P(None, ALL),
        ),
        out_specs=(P(DP, "tensor"), P()),
        check_vma=False,
    )
```

time: 693 us -> 231 us (0.33)
  waiting for transfers between devices: 386 us -> 18.1 us
  blocking collectives: 138 us -> 43.7 us
  matrix products: 84.8 us -> 0 us
  Pallas kernels: 0 us -> 76 us
  starting transfers between devices: 8.43 us -> 44.3 us
  other arithmetic: 37.5 us -> 6.5 us
  local copies, waits for them, and re-layouts: 21.5 us -> 40 us
  between operations: 16.2 us -> 1.46 us
    all_gather x1 -> x0, waiting for transfers between devices: 331 us -> none  [on_device(): piece = lax.all_gather(w_head, 'dp', axis=1, tiled=True)]
    pallas_call x0 -> x19, Pallas kernels: none -> 76 us  [the longest x4 49.4 us: head_stats(): pl.pallas_call(body, grid=(steps,), out_shape=jax.ShapeDtypeStruct((8, co...]
    dot_general x17 -> x0, matrix products: 75.3 us -> none  [the longest x1 39.9 us: on_device(): logits = jnp.dot(rows_all, piece, preferred_element_type=jnp.float32)]
    reduce_scatter x2 -> x0, waiting for transfers between devices: 54.1 us -> none  [on_device(): lax.psum_scatter(partial_value.reshape(slots, block_len, width), 'tensor'...]
    all_gather x8 -> x3, blocking collectives: 82.4 us -> 34.8 us  [the longest x2 20.9 us: on_device(): kv = lax.all_gather(kv, 'tensor', axis=1, tiled=True)]
    psum x2 -> x0, blocking collectives: 45.7 us -> none  [the longest x1 37.8 us: on_device(): doc_total = lax.psum(partial_docs, ('dp', 'tensor'))]
    unnamed x45 -> x92, local copies, waits for them, and re-layouts: 1.03 us -> 32.7 us
    ppermute x4 -> x30, starting transfers between devices: 8.31 us -> 38.8 us  [the longest x21 25.1 us: peer(): return lax.ppermute(x, 'tensor', [(i, i ^ k) for i in range(tp_count)])]
  transfers between devices with their start and end apart: 7 -> 31, of which waited for: 3 -> 4; matrix products, arithmetic and copies ran while one was open for 3% -> 3% of each run, Pallas kernels for 0% -> 27%
where the time goes in v1:
time: 231 us; the launch traced here: 230 us
  Pallas kernels  76 us (33%)
  starting transfers between devices  44.3 us (19%)
  blocking collectives  43.7 us (19%)
  local copies, waits for them, and re-layouts  40 us (17%)
  waiting for transfers between devices  18.1 us (8%)
  other arithmetic  6.5 us (3%)
    pallas_call x4, Pallas kernels, head_stats(): pl.pallas_call(body, grid=(steps,), out_shape=jax.ShapeDtypeStruct((8, co...  49.4 us
    unnamed x92, local copies, waits for them, and re-layouts  32.7 us
    ppermute x21, starting transfers between devices, peer(): return lax.ppermute(x, 'tensor', [(i, i ^ k) for i in range(tp_count)])  25.1 us
    all_gather x2, blocking collectives, on_device(): kv = lax.all_gather(kv, 'tensor', axis=1, tiled=True)  20.9 us
    pallas_call x8, Pallas kernels, mlp(): pl.pallas_call(body, grid=(1,), out_shape=jax.ShapeDtypeStruct((count, wi...  18.6 us
    all_gather x1, blocking collectives, on_device(): first = lax.all_gather(final, 'tensor', axis=0, tiled=True)  14 us
    ppermute x8, starting transfers between devices, shift(): return lax.ppermute(x, axes, pairs)  11.6 us
    ppermute x21, waiting for transfers between devices, peer(): return lax.ppermute(x, 'tensor', [(i, i ^ k) for i in range(tp_count)])  10.7 us
  transfers between devices with their start and end apart: 31, of which 4 were waited for; matrix products, arithmetic and copies ran while one was open for 3% of the time, Pallas kernels for 27%

profile of v1, /device:TPU:0, one launch (start us, length us, event | category | flops | bytes accessed | tf_op | source)
XLA Modules:
  0.0 230.0 jit_solution(4264695816521423427)
XLA Ops:
  8.9 3.0 %collective-permute-start = (bf16[3,32,256]{2,1,0:T(8,128)(2,1)}, bf16[3,32,256]{2,1,0:T(8,128)(2,1)}, u32[]{:S(2)}, u32[]{:S(2)}) collective-permute-start(bf16[3,32,256]{2,1,0:T(8,128)(2,1)} %bitcast.4), channel_id=1, source_target_pairs={{0,4},{4,8},{8,12},{12,16},{16,20},{20,24},{24,28},{1,5},{5,9},{9,... | collective-permute-start | bytes 147464 | tf_op jit(solution)/shard_map/ppermute | solution.py:375
  11.9 2.1 collective-permute-start.14
  21.4 10.0 %all_gather.9 = bf16[8,128,256]{2,1,0:T(8,128)(2,1)S(1)} all-gather(bf16[8,32,256]{2,1,0:T(8,128)(2,1)S(1)} %pad_maximum_fusion), channel_id=1, replica_groups=mesh['zp'=2,'zq'=2,'core'=2,'tensor'=4] {'tensor'}, dimensions={1}, use_global_device_ids=true | all-gather | bytes 655360 | tf_op jit(solution)/shard_map/all_gather | solution.py:465
  32.3 2.9 %attention.2 = (f32[128,896]{1,0:T(8,128)S(1)}, bf16[128,896]{1,0:T(8,128)(2,1)}) custom-call(bf16[128,896]{1,0:T(8,128)(2,1)S(1)} %queries.2.q_ref, bf16[896,256]{1,0:T(8,128)(2,1)S(1)} %bitcast.82, f32[4,32,512]{2,1,0:T(8,128)S(1)} %and_select_fusion.bias_ref, f32[128,896]{1,0:T(8,128)S(1)} %copy-done.24, bf16[2,896,896]{2,1,0:T(8,128)(2,1)S(1)} %copy-done.9, ...), custom_call_target="tpu_custom_call" | custom-call | flops 675282944 | tf_op jit(solution)/shard_map/attention/pallas_call | solution.py:229
  40.7 3.6 %collective-permute-done.1.x_ref = bf16[128,896]{1,0:T(8,128)(2,1)} collective-permute-done((bf16[128,896]{1,0:T(8,128)(2,1)}, bf16[128,896]{1,0:T(8,128)(2,1)}, u32[]{:S(2)}, u32[]{:S(2)}) %collective-permute-start.1) | collective-permute-done | bytes 229408 | tf_op jit(solution)/shard_map/ppermute | solution.py:413
  44.2 2.2 copy-done
  46.5 2.2 copy-done.3
  48.7 2.2 copy-done.6
  50.9 2.8 %mlp.9 = bf16[128,896]{1,0:T(8,128)(2,1)S(1)} custom-call(bf16[128,896]{1,0:T(8,128)(2,1)} %collective-permute-done.1.x_ref, bf16[2,1216,896]{2,1,0:T(8,128)(2,1)S(1)} %bitcast.64, bf16[2,1216,896]{2,1,0:T(8,128)(2,1)S(1)} %bitcast.74, bf16[2,1216,896]{2,1,0:T(8,128)(2,1)S(1)} %copy-done.6), custom_call_target="tpu_custom_call" | custom-call | flops 836763648 | tf_op jit(solution)/shard_map/mlp/pallas_call | solution.py:257
  55.4 2.9 %mlp.10 = bf16[128,896]{1,0:T(8,128)(2,1)S(1)} custom-call(bf16[128,896]{1,0:T(8,128)(2,1)} %collective-permute-done.3.x_ref, bf16[2,1216,896]{2,1,0:T(8,128)(2,1)S(1)} %bitcast.65, bf16[2,1216,896]{2,1,0:T(8,128)(2,1)S(1)} %bitcast.75, bf16[2,1216,896]{2,1,0:T(8,128)(2,1)S(1)} %copy-done.6), custom_call_target="tpu_custom_call" | custom-call | flops 836763648 | tf_op jit(solution)/shard_map/mlp/pallas_call | solution.py:257
  62.2 2.9 %mlp.8.refs_1_ = f32[128,896]{1,0:T(8,128)S(1)} custom-call(bf16[128,896]{1,0:T(8,128)(2,1)} %get-tuple-element.19.x_ref, bf16[2,1216,896]{2,1,0:T(8,128)(2,1)S(1)} %bitcast.69, bf16[2,1216,896]{2,1,0:T(8,128)(2,1)S(1)} %bitcast.77, bf16[2,1216,896]{2,1,0:T(8,128)(2,1)S(1)} %copy-done.6), custom_call_target="tpu_custom_call" | custom-call | flops 836763648 | tf_op jit(solution)/shard_map/mlp/pallas_call | solution.py:257
  65.2 2.5 %collective-permute-done.6.refs_4_ = bf16[128,896]{1,0:T(8,128)(2,1)S(1)} collective-permute-done((bf16[128,896]{1,0:T(8,128)(2,1)S(1)}, bf16[128,896]{1,0:T(8,128)(2,1)S(1)}, u32[]{:S(2)}, u32[]{:S(2)}) %collective-permute-start.6) | collective-permute-done | bytes 229408 | tf_op jit(solution)/shard_map/ppermute | solution.py:413
  70.1 3.2 %collective-permute-start.15 = (s32[4,128]{1,0:T(4,128)}, s32[4,128]{1,0:T(4,128)}, u32[]{:S(2)}, u32[]{:S(2)}) collective-permute-start(s32[4,128]{1,0:T(4,128)} %bitcast.22), channel_id=1, source_target_pairs={{0,16},{16,0},{1,17},{17,1},{2,18},{18,2},{3,19},{19,3},{4,20},{20... | collective-permute-start | bytes 6152 | tf_op jit(solution)/shard_map/ppermute | solution.py:375
  74.0 10.8 %all_gather.10 = bf16[7,128,256]{2,1,0:T(8,128)(2,1)S(1)} all-gather(bf16[7,32,256]{2,1,0:T(8,128)(2,1)S(1)} %pad_maximum_fusion.1), channel_id=1, replica_groups=mesh['zp'=2,'zq'=2,'core'=2,'tensor'=4] {'tensor'}, dimensions={1}, use_global_device_ids=true | all-gather | bytes 573440 | tf_op jit(solution)/shard_map/all_gather | solution.py:465
  84.8 2.9 %attention.3 = (f32[128,896]{1,0:T(8,128)S(1)}, bf16[128,896]{1,0:T(8,128)(2,1)}) custom-call(bf16[128,896]{1,0:T(8,128)(2,1)S(1)} %queries.3.q_ref, bf16[896,256]{1,0:T(8,128)(2,1)S(1)} %bitcast.83, f32[4,32,512]{2,1,0:T(8,128)S(1)} %and_select_fusion.bias_ref, f32[128,896]{1,0:T(8,128)S(1)} %get-tuple-element.22.h_ref, bf16[2,896,896]{2,1,0:T(8,128)(2,1)S(1)} %copy-done.9, ...), custom_call_target="tpu_custom_call" | custom-call | flops 675282944 | tf_op jit(solution)/shard_map/attention/pallas_call | solution.py:229
  95.2 4.6 %collective-permute-done.10.x_ref = bf16[128,896]{1,0:T(8,128)(2,1)S(1)} collective-permute-done((bf16[128,896]{1,0:T(8,128)(2,1)}, bf16[128,896]{1,0:T(8,128)(2,1)S(1)}, u32[]{:S(2)}, u32[]{:S(2)}) %collective-permute-start.10) | collective-permute-done | bytes 229408 | tf_op jit(solution)/shard_map/ppermute | solution.py:413
  99.8 2.2 copy-done.1
  102.0 2.2 copy-done.4
  104.2 2.2 copy-done.7
  116.0 2.2 copy-done.2
  118.2 2.2 copy-done.5
  120.4 2.2 copy-done.8
  122.7 2.8 %mlp.12.refs_0_ = f32[128,896]{1,0:T(8,128)S(1)} custom-call(bf16[128,896]{1,0:T(8,128)(2,1)} %get-tuple-element.24.x_ref, bf16[2,1216,896]{2,1,0:T(8,128)(2,1)S(1)} %bitcast.73, bf16[2,1216,896]{2,1,0:T(8,128)(2,1)S(1)} %bitcast.81, bf16[2,1216,896]{2,1,0:T(8,128)(2,1)S(1)} %copy-done.8), custom_call_target="tpu_custom_call" | custom-call | flops 836763648 | tf_op jit(solution)/shard_map/mlp/pallas_call | solution.py:257
  126.5 14.0 %all_gather.11.rest_0_ = bf16[512,896]{1,0:T(8,128)(2,1)S(1)} all-gather(bf16[128,896]{1,0:T(8,128)(2,1)S(1)} %last_norm.1), channel_id=1, replica_groups=mesh['zp'=2,'zq'=2,'core'=2,'tensor'=4] {'tensor'}, dimensions={0}, use_global_device_ids=true | all-gather | bytes 1146880 | tf_op jit(solution)/shard_map/all_gather | solution.py:505
  145.3 2.6 %copy-done.33 = bf16[896,3072]{1,0:T(8,128)(2,1)S(1)} copy-done((bf16[896,3072]{1,0:T(8,128)(2,1)S(1)}, bf16[896,3072]{1,0:T(8,128)(2,1)}, u32[]{:S(2)}) %copy-start.33) | copy-done | bytes 5505048
  147.9 12.3 %head_stats.4 = f32[8,512]{1,0:T(8,128)S(1)} custom-call(s32[2]{0:T(128)S(1)} %pad_add_fusion.4.base_ref, s32[512,1]{1,0:T(8,128)S(1)} %copy.54.want_ref, bf16[512,896]{1,0:T(8,128)(2,1)S(1)} %all_gather.11.rest_0_, bf16[896,3072]{1,0:T(8,128)(2,1)S(1)} %copy-done.33, bf16[896,3072]{1,0:T(8,128)(2,1)} %collective-permute-done.14.rest_2_.rest_5_), custom_call_target="tpu_custom_call" | custom-call | flops 5637144576 | tf_op jit(solution)/shard_map/head_stats/pallas_call | solution.py:354
  163.7 12.3 %head_stats.5 = f32[8,512]{1,0:T(8,128)S(1)} custom-call(s32[2]{0:T(128)S(1)} %pad_add_fusion.4.base_ref, s32[512,1]{1,0:T(8,128)S(1)} %copy.55.want_ref, bf16[128,896]{1,0:T(8,128)(2,1)S(1)} %collective-permute-done.16.rest_0_, bf16[128,896]{1,0:T(8,128)(2,1)S(1)} %collective-permute-done.17.rest_1_, bf16[128,896]{1,0:T(8,128)(2,1)S(1)} %collective-permute-done.18.rest_2_, ...), custom_call_target="tpu_custom_call" | custom-call | flops 5637144576 | tf_op jit(solution)/shard_map/head_stats/pallas_call | solution.py:354
  179.6 12.3 %head_stats.6 = f32[8,512]{1,0:T(8,128)S(1)} custom-call(s32[2]{0:T(128)S(1)} %pad_add_fusion.4.base_ref, s32[512,1]{1,0:T(8,128)S(1)} %copy.56.want_ref, bf16[128,896]{1,0:T(8,128)(2,1)S(1)} %collective-permute-done.21.rest_0_, bf16[128,896]{1,0:T(8,128)(2,1)S(1)} %collective-permute-done.22.rest_1_, bf16[128,896]{1,0:T(8,128)(2,1)S(1)} %collective-permute-done.23.rest_2_, ...), custom_call_target="tpu_custom_call" | custom-call | flops 5637144576 | tf_op jit(solution)/shard_map/head_stats/pallas_call | solution.py:354
  192.0 12.6 %head_stats.7 = f32[8,512]{1,0:T(8,128)S(1)} custom-call(s32[2]{0:T(128)S(1)} %pad_add_fusion.4.base_ref, s32[512,1]{1,0:T(8,128)S(1)} %copy.57.want_ref, bf16[128,896]{1,0:T(8,128)(2,1)S(1)} %collective-permute-done.26.rest_0_, bf16[128,896]{1,0:T(8,128)(2,1)S(1)} %collective-permute-done.27.rest_1_, bf16[128,896]{1,0:T(8,128)(2,1)S(1)} %collective-permute-done.28.rest_2_, ...), custom_call_target="tpu_custom_call" | custom-call | flops 5637144576 | tf_op jit(solution)/shard_map/head_stats/pallas_call | solution.py:354
  207.3 5.5 %all-to-all-start = ((f32[16,3,128]{2,1,0:T(4,128)}), f32[16,3,128]{2,1,0:T(4,128)S(1)}, u32[]{:S(2)}, u32[]{:S(2)}) async-start(f32[16,3,128]{2,1,0:T(4,128)} %copy.60), calls=%async_computation | async-start | bytes 65536 | tf_op jit(solution)/shard_map/all_to_all | solution.py:534
  212.8 7.4 %all-to-all-done = f32[16,3,128]{2,1,0:T(4,128)S(1)} async-done(((f32[16,3,128]{2,1,0:T(4,128)}), f32[16,3,128]{2,1,0:T(4,128)S(1)}, u32[]{:S(2)}, u32[]{:S(2)}) %all-to-all-start) | async-done | bytes 24608 | tf_op jit(solution)/shard_map/all_to_all | solution.py:534
  220.6 8.9 %all_to_all.11 = f32[32,1,128]{2,1,0:T(1,128)S(1)} all-to-all(f32[32,1,128]{2,1,0:T(1,128)S(1)} %broadcast_in_dim.180), channel_id=1, replica_groups=mesh['zp'=2,'zq'=2,'core'=2,'tensor'=4] {'zp','zq','core','tensor'}, dimensions={0} | all-to-all | bytes 32768 | tf_op jit(solution)/shard_map/all_to_all | solution.py:545
  (229 shorter events, 63.8 us)
Async XLA Ops:
  8.9 11.7 %collective-permute-start = (bf16[3,32,256]{2,1,0:T(8,128)(2,1)}, bf16[3,32,256]{2,1,0:T(8,128)(2,1)}, u32[]{:S(2)}, u32[]{:S(2)}) collective-permute-start(bf16[3,32,256]{2,1,0:T(8,128)(2,1)} %bitcast.4), channel_id=1, source_target_pairs={{0,4},{4,8},{8,12},{12,16},{16,20},{20,24},{24,28},{1,5},{5,9},{9,... | collective-permute-start | bytes 147464 | tf_op jit(solution)/shard_map/ppermute | solution.py:375
  11.9 132.1 %collective-permute-start.14 = (bf16[896,3072]{1,0:T(8,128)(2,1)}, bf16[896,3072]{1,0:T(8,128)(2,1)}, u32[]{:S(2)}, u32[]{:S(2)}) collective-permute-start(bf16[896,3072]{1,0:T(8,128)(2,1)} %rest_4_.5), channel_id=1, source_target_pairs={{0,4},{4,0},{1,5},{5,1},{2,6},{6,2},{3,7},{7,3},{8,12},{12,8},{9,1... | collective-permute-start | bytes 16515080 | tf_op jit(solution)/shard_map/ppermute | solution.py:417
  36.0 8.3 %collective-permute-start.1 = (bf16[128,896]{1,0:T(8,128)(2,1)}, bf16[128,896]{1,0:T(8,128)(2,1)}, u32[]{:S(2)}, u32[]{:S(2)}) collective-permute-start(bf16[128,896]{1,0:T(8,128)(2,1)} %get-tuple-element.19.x_ref), channel_id=1, source_target_pairs={{0,1},{1,0},{2,3},{3,2},{4,5},{5,4},{6,7},{7,6},{8,9},{9,8},{10,11... | collective-permute-start | bytes 688136 | tf_op jit(solution)/shard_map/ppermute | solution.py:413
  38.0 17.3 %collective-permute-start.3 = (bf16[128,896]{1,0:T(8,128)(2,1)}, bf16[128,896]{1,0:T(8,128)(2,1)}, u32[]{:S(2)}, u32[]{:S(2)}) collective-permute-start(bf16[128,896]{1,0:T(8,128)(2,1)} %get-tuple-element.19.x_ref), channel_id=1, source_target_pairs={{0,2},{1,3},{2,0},{3,1},{4,6},{5,7},{6,4},{7,5},{8,10},{9,11},{10,... | collective-permute-start | bytes 688136 | tf_op jit(solution)/shard_map/ppermute | solution.py:413
  39.1 19.7 %collective-permute-start.5 = (bf16[128,896]{1,0:T(8,128)(2,1)}, bf16[128,896]{1,0:T(8,128)(2,1)S(1)}, u32[]{:S(2)}, u32[]{:S(2)}) collective-permute-start(bf16[128,896]{1,0:T(8,128)(2,1)} %get-tuple-element.19.x_ref), channel_id=1, source_target_pairs={{0,3},{1,2},{2,1},{3,0},{4,7},{5,6},{6,5},{7,4},{8,11},{9,10},{10,... | collective-permute-start | bytes 688136 | tf_op jit(solution)/shard_map/ppermute | solution.py:413
  53.7 11.5 %collective-permute-start.2 = (bf16[128,896]{1,0:T(8,128)(2,1)S(1)}, bf16[128,896]{1,0:T(8,128)(2,1)S(1)}, u32[]{:S(2)}, u32[]{:S(2)}) collective-permute-start(bf16[128,896]{1,0:T(8,128)(2,1)S(1)} %mlp.9), channel_id=1, source_target_pairs={{0,1},{1,0},{2,3},{3,2},{4,5},{5,4},{6,7},{7,6},{8,9},{9,8},{10,11... | collective-permute-start | bytes 688136 | tf_op jit(solution)/shard_map/ppermute | solution.py:413
  58.3 6.9 %collective-permute-start.4 = (bf16[128,896]{1,0:T(8,128)(2,1)S(1)}, bf16[128,896]{1,0:T(8,128)(2,1)S(1)}, u32[]{:S(2)}, u32[]{:S(2)}) collective-permute-start(bf16[128,896]{1,0:T(8,128)(2,1)S(1)} %mlp.10), channel_id=1, source_target_pairs={{0,2},{1,3},{2,0},{3,1},{4,6},{5,7},{6,4},{7,5},{8,10},{9,11},{10,... | collective-permute-start | bytes 688136 | tf_op jit(solution)/shard_map/ppermute | solution.py:413
  60.7 7.0 %collective-permute-start.6 = (bf16[128,896]{1,0:T(8,128)(2,1)S(1)}, bf16[128,896]{1,0:T(8,128)(2,1)S(1)}, u32[]{:S(2)}, u32[]{:S(2)}) collective-permute-start(bf16[128,896]{1,0:T(8,128)(2,1)S(1)} %mlp.11), channel_id=1, source_target_pairs={{0,3},{1,2},{2,1},{3,0},{4,7},{5,6},{6,5},{7,4},{8,11},{9,10},{10,... | collective-permute-start | bytes 688136 | tf_op jit(solution)/shard_map/ppermute | solution.py:413
  68.2 5.7 %collective-permute-start.7 = (bf16[3,32,256]{2,1,0:T(8,128)(2,1)S(1)}, bf16[3,32,256]{2,1,0:T(8,128)(2,1)S(1)}, u32[]{:S(2)}, u32[]{:S(2)}) collective-permute-start(bf16[3,32,256]{2,1,0:T(8,128)(2,1)S(1)} %bitcast.99), channel_id=1, source_target_pairs={{0,4},{4,8},{8,12},{12,16},{16,20},{20,24},{24,28},{1,5},{5,9},{9,... | collective-permute-start | bytes 147464 | tf_op jit(solution)/shard_map/ppermute | solution.py:375
  70.1 19.7 %collective-permute-start.15 = (s32[4,128]{1,0:T(4,128)}, s32[4,128]{1,0:T(4,128)}, u32[]{:S(2)}, u32[]{:S(2)}) collective-permute-start(s32[4,128]{1,0:T(4,128)} %bitcast.22), channel_id=1, source_target_pairs={{0,16},{16,0},{1,17},{17,1},{2,18},{18,2},{3,19},{19,3},{4,20},{20... | collective-permute-start | bytes 6152 | tf_op jit(solution)/shard_map/ppermute | solution.py:375
  88.5 11.3 %collective-permute-start.10 = (bf16[128,896]{1,0:T(8,128)(2,1)}, bf16[128,896]{1,0:T(8,128)(2,1)S(1)}, u32[]{:S(2)}, u32[]{:S(2)}) collective-permute-start(bf16[128,896]{1,0:T(8,128)(2,1)} %get-tuple-element.24.x_ref), channel_id=1, source_target_pairs={{0,2},{1,3},{2,0},{3,1},{4,6},{5,7},{6,4},{7,5},{8,10},{9,11},{10,... | collective-permute-start | bytes 688136 | tf_op jit(solution)/shard_map/ppermute | solution.py:413
  89.1 4.6 %collective-permute-start.20 = (s32[4,128]{1,0:T(4,128)}, s32[4,128]{1,0:T(4,128)S(1)}, u32[]{:S(2)}, u32[]{:S(2)}) collective-permute-start(s32[4,128]{1,0:T(4,128)} %bitcast.22), channel_id=1, source_target_pairs={{0,8},{8,0},{1,9},{9,1},{2,10},{10,2},{3,11},{11,3},{4,12},{12,4},... | collective-permute-start | bytes 6152 | tf_op jit(solution)/shard_map/ppermute | solution.py:375
  89.8 26.1 %collective-permute-start.25 = (s32[4,128]{1,0:T(4,128)}, s32[4,128]{1,0:T(4,128)S(1)}, u32[]{:S(2)}, u32[]{:S(2)}) collective-permute-start(s32[4,128]{1,0:T(4,128)} %collective-permute-done.15), channel_id=1, source_target_pairs={{0,8},{8,0},{1,9},{9,1},{2,10},{10,2},{3,11},{11,3},{4,12},{12,4},... | collective-permute-start | bytes 6152 | tf_op jit(solution)/shard_map/ppermute | solution.py:375
  91.5 17.3 %collective-permute-start.12 = (bf16[128,896]{1,0:T(8,128)(2,1)}, bf16[128,896]{1,0:T(8,128)(2,1)S(1)}, u32[]{:S(2)}, u32[]{:S(2)}) collective-permute-start(bf16[128,896]{1,0:T(8,128)(2,1)} %get-tuple-element.24.x_ref), channel_id=1, source_target_pairs={{0,3},{1,2},{2,1},{3,0},{4,7},{5,6},{6,5},{7,4},{8,11},{9,10},{10,... | collective-permute-start | bytes 688136 | tf_op jit(solution)/shard_map/ppermute | solution.py:413
  93.8 18.4 %collective-permute-start.8 = (bf16[128,896]{1,0:T(8,128)(2,1)}, bf16[128,896]{1,0:T(8,128)(2,1)S(1)}, u32[]{:S(2)}, u32[]{:S(2)}) collective-permute-start(bf16[128,896]{1,0:T(8,128)(2,1)} %get-tuple-element.24.x_ref), channel_id=1, source_target_pairs={{0,1},{1,0},{2,3},{3,2},{4,5},{5,4},{6,7},{7,6},{8,9},{9,8},{10,11... | collective-permute-start | bytes 688136 | tf_op jit(solution)/shard_map/ppermute | solution.py:413
  108.3 17.2 %collective-permute-start.11 = (bf16[128,896]{1,0:T(8,128)(2,1)S(1)}, bf16[128,896]{1,0:T(8,128)(2,1)S(1)}, u32[]{:S(2)}, u32[]{:S(2)}) collective-permute-start(bf16[128,896]{1,0:T(8,128)(2,1)S(1)} %mlp.14), channel_id=1, source_target_pairs={{0,2},{1,3},{2,0},{3,1},{4,6},{5,7},{6,4},{7,5},{8,10},{9,11},{10,... | collective-permute-start | bytes 688136 | tf_op jit(solution)/shard_map/ppermute | solution.py:413
  110.6 14.9 %collective-permute-start.13 = (bf16[128,896]{1,0:T(8,128)(2,1)S(1)}, bf16[128,896]{1,0:T(8,128)(2,1)S(1)}, u32[]{:S(2)}, u32[]{:S(2)}) collective-permute-start(bf16[128,896]{1,0:T(8,128)(2,1)S(1)} %mlp.15), channel_id=1, source_target_pairs={{0,3},{1,2},{2,1},{3,0},{4,7},{5,6},{6,5},{7,4},{8,11},{9,10},{10,... | collective-permute-start | bytes 688136 | tf_op jit(solution)/shard_map/ppermute | solution.py:413
  113.9 11.6 %collective-permute-start.9 = (bf16[128,896]{1,0:T(8,128)(2,1)S(1)}, bf16[128,896]{1,0:T(8,128)(2,1)S(1)}, u32[]{:S(2)}, u32[]{:S(2)}) collective-permute-start(bf16[128,896]{1,0:T(8,128)(2,1)S(1)} %mlp.13), channel_id=1, source_target_pairs={{0,1},{1,0},{2,3},{3,2},{4,5},{5,4},{6,7},{7,6},{8,9},{9,8},{10,11... | collective-permute-start | bytes 688136 | tf_op jit(solution)/shard_map/ppermute | solution.py:413
  125.7 14.7 %collective-permute-start.16 = (bf16[128,896]{1,0:T(8,128)(2,1)S(1)}, bf16[128,896]{1,0:T(8,128)(2,1)S(1)}, u32[]{:S(2)}, u32[]{:S(2)}) collective-permute-start(bf16[128,896]{1,0:T(8,128)(2,1)S(1)} %last_norm.1), channel_id=1, source_target_pairs={{0,16},{16,0},{1,17},{17,1},{2,18},{18,2},{3,19},{19,3},{4,20},{20... | collective-permute-start | bytes 688136 | tf_op jit(solution)/shard_map/ppermute | solution.py:375
  126.0 34.2 %collective-permute-start.21 = (bf16[128,896]{1,0:T(8,128)(2,1)S(1)}, bf16[128,896]{1,0:T(8,128)(2,1)S(1)}, u32[]{:S(2)}, u32[]{:S(2)}) collective-permute-start(bf16[128,896]{1,0:T(8,128)(2,1)S(1)} %last_norm.1), channel_id=1, source_target_pairs={{0,8},{8,0},{1,9},{9,1},{2,10},{10,2},{3,11},{11,3},{4,12},{12,4},... | collective-permute-start | bytes 688136 | tf_op jit(solution)/shard_map/ppermute | solution.py:375
  140.4 21.6 %collective-permute-start.17 = (bf16[128,896]{1,0:T(8,128)(2,1)S(1)}, bf16[128,896]{1,0:T(8,128)(2,1)S(1)}, u32[]{:S(2)}, u32[]{:S(2)}) collective-permute-start(bf16[128,896]{1,0:T(8,128)(2,1)S(1)} %collective-permute-done.16.rest_0_), channel_id=1, source_target_pairs={{0,1},{1,0},{2,3},{3,2},{4,5},{5,4},{6,7},{7,6},{8,9},{9,8},{10,11... | collective-permute-start | bytes 688136 | tf_op jit(solution)/shard_map/ppermute | solution.py:413
  141.7 20.6 %collective-permute-start.18 = (bf16[128,896]{1,0:T(8,128)(2,1)S(1)}, bf16[128,896]{1,0:T(8,128)(2,1)S(1)}, u32[]{:S(2)}, u32[]{:S(2)}) collective-permute-start(bf16[128,896]{1,0:T(8,128)(2,1)S(1)} %collective-permute-done.16.rest_0_), channel_id=1, source_target_pairs={{0,2},{1,3},{2,0},{3,1},{4,6},{5,7},{6,4},{7,5},{8,10},{9,11},{10,... | collective-permute-start | bytes 688136 | tf_op jit(solution)/shard_map/ppermute | solution.py:413
  142.5 21.2 %collective-permute-start.19 = (bf16[128,896]{1,0:T(8,128)(2,1)S(1)}, bf16[128,896]{1,0:T(8,128)(2,1)S(1)}, u32[]{:S(2)}, u32[]{:S(2)}) collective-permute-start(bf16[128,896]{1,0:T(8,128)(2,1)S(1)} %collective-permute-done.16.rest_0_), channel_id=1, source_target_pairs={{0,3},{1,2},{2,1},{3,0},{4,7},{5,6},{6,5},{7,4},{8,11},{9,10},{10,... | collective-permute-start | bytes 688136 | tf_op jit(solution)/shard_map/ppermute | solution.py:413
  144.0 32.0 %collective-permute-start.26 = (bf16[128,896]{1,0:T(8,128)(2,1)S(1)}, bf16[128,896]{1,0:T(8,128)(2,1)S(1)}, u32[]{:S(2)}, u32[]{:S(2)}) collective-permute-start(bf16[128,896]{1,0:T(8,128)(2,1)S(1)} %collective-permute-done.16.rest_0_), channel_id=1, source_target_pairs={{0,8},{8,0},{1,9},{9,1},{2,10},{10,2},{3,11},{11,3},{4,12},{12,4},... | collective-permute-start | bytes 688136 | tf_op jit(solution)/shard_map/ppermute | solution.py:375
  160.2 18.0 %collective-permute-start.22 = (bf16[128,896]{1,0:T(8,128)(2,1)S(1)}, bf16[128,896]{1,0:T(8,128)(2,1)S(1)}, u32[]{:S(2)}, u32[]{:S(2)}) collective-permute-start(bf16[128,896]{1,0:T(8,128)(2,1)S(1)} %collective-permute-done.21.rest_0_), channel_id=1, source_target_pairs={{0,1},{1,0},{2,3},{3,2},{4,5},{5,4},{6,7},{7,6},{8,9},{9,8},{10,11... | collective-permute-start | bytes 688136 | tf_op jit(solution)/shard_map/ppermute | solution.py:413
  162.0 17.6 %collective-permute-start.23 = (bf16[128,896]{1,0:T(8,128)(2,1)S(1)}, bf16[128,896]{1,0:T(8,128)(2,1)S(1)}, u32[]{:S(2)}, u32[]{:S(2)}) collective-permute-start(bf16[128,896]{1,0:T(8,128)(2,1)S(1)} %collective-permute-done.21.rest_0_), channel_id=1, source_target_pairs={{0,2},{1,3},{2,0},{3,1},{4,6},{5,7},{6,4},{7,5},{8,10},{9,11},{10,... | collective-permute-start | bytes 688136 | tf_op jit(solution)/shard_map/ppermute | solution.py:413
  162.3 17.3 %collective-permute-start.24 = (bf16[128,896]{1,0:T(8,128)(2,1)S(1)}, bf16[128,896]{1,0:T(8,128)(2,1)S(1)}, u32[]{:S(2)}, u32[]{:S(2)}) collective-permute-start(bf16[128,896]{1,0:T(8,128)(2,1)S(1)} %collective-permute-done.21.rest_0_), channel_id=1, source_target_pairs={{0,3},{1,2},{2,1},{3,0},{4,7},{5,6},{6,5},{7,4},{8,11},{9,10},{10,... | collective-permute-start | bytes 688136 | tf_op jit(solution)/shard_map/ppermute | solution.py:413
  176.0 15.9 %collective-permute-start.27 = (bf16[128,896]{1,0:T(8,128)(2,1)S(1)}, bf16[128,896]{1,0:T(8,128)(2,1)S(1)}, u32[]{:S(2)}, u32[]{:S(2)}) collective-permute-start(bf16[128,896]{1,0:T(8,128)(2,1)S(1)} %collective-permute-done.26.rest_0_), channel_id=1, source_target_pairs={{0,1},{1,0},{2,3},{3,2},{4,5},{5,4},{6,7},{7,6},{8,9},{9,8},{10,11... | collective-permute-start | bytes 688136 | tf_op jit(solution)/shard_map/ppermute | solution.py:413
  177.9 14.1 %collective-permute-start.28 = (bf16[128,896]{1,0:T(8,128)(2,1)S(1)}, bf16[128,896]{1,0:T(8,128)(2,1)S(1)}, u32[]{:S(2)}, u32[]{:S(2)}) collective-permute-start(bf16[128,896]{1,0:T(8,128)(2,1)S(1)} %collective-permute-done.26.rest_0_), channel_id=1, source_target_pairs={{0,2},{1,3},{2,0},{3,1},{4,6},{5,7},{6,4},{7,5},{8,10},{9,11},{10,... | collective-permute-start | bytes 688136 | tf_op jit(solution)/shard_map/ppermute | solution.py:413
  178.1 13.8 %collective-permute-start.29 = (bf16[128,896]{1,0:T(8,128)(2,1)S(1)}, bf16[128,896]{1,0:T(8,128)(2,1)S(1)}, u32[]{:S(2)}, u32[]{:S(2)}) collective-permute-start(bf16[128,896]{1,0:T(8,128)(2,1)S(1)} %collective-permute-done.26.rest_0_), channel_id=1, source_target_pairs={{0,3},{1,2},{2,1},{3,0},{4,7},{5,6},{6,5},{7,4},{8,11},{9,10},{10,... | collective-permute-start | bytes 688136 | tf_op jit(solution)/shard_map/ppermute | solution.py:413
  191.9 37.5 %copy-start.40 = (s32[16]{0:T(128)S(1)}, s32[16]{0:T(128)}, u32[]{:S(2)}) copy-start(s32[16]{0:T(128)} %param.17) | copy-start | bytes 196
  207.3 12.9 %all-to-all-start = ((f32[16,3,128]{2,1,0:T(4,128)}), f32[16,3,128]{2,1,0:T(4,128)S(1)}, u32[]{:S(2)}, u32[]{:S(2)}) async-start(f32[16,3,128]{2,1,0:T(4,128)} %copy.60), calls=%async_computation | async-start | bytes 65536 | tf_op jit(solution)/shard_map/all_to_all | solution.py:534
  (45 other events, 284.0 us)

commit v2 on v1

--- a/solution.py
+++ b/solution.py
@@ -61,6 +61,10 @@
 def layer_of(array, layer):
     shape = array.shape[1:]
     return pl.BlockSpec((None,) + shape, lambda *_: (layer,) + (0,) * len(shape))
+
+
+def in_hbm(x):
+    return pltpu.with_memory_space_constraint(x, pltpu.HBM)
 
 
 def cost(flops, moved):
@@ -108,7 +112,7 @@
             kv_out[:, at * LANES : (at + 1) * LANES] = piece.astype(BF16)
         kv_out[:, kvw:] = dot(a, wv_ref[...]).astype(BF16)
 
-    args = [h] + parts + [gains, w_key, w_value, cosine, sine]
+    args = [h] + parts + [gains, in_hbm(w_key), in_hbm(w_value), cosine, sine]
     specs = [whole(x.shape) for x in args]
     specs[-5] = layer_of(gains, layer)
     specs[-4] = layer_of(w_key, layer)
@@ -154,14 +158,14 @@
         compiler_params=params(10),
         cost_estimate=cost(2.0 * count * out * out, 0),
         name="queries",
-    )(a, w_query, cosine, sine)
-
-
-def attention(q, kv, bias, h, w_out, gains, layer):
+    )(a, in_hbm(w_query), cosine, sine)
+
+
+def attention(q, tail_pieces, own_pieces, bias, h, w_out, gains, layer):
     blocks, rows, span = bias.shape
     count, qw = q.shape
     width = h.shape[1]
-    kvw = kv.shape[1] // 2
+    kvw = own_pieces[0].shape[1] // 2
     kvh = kvw // HEAD_DIM
     heads = qw // HEAD_DIM
     group = heads // kvh
@@ -169,7 +173,22 @@
     block_len = span // MAXB
     assert kvw == LANES and kvh == 2
 
-    def body(q_ref, kv_ref, bias_ref, h_ref, wo_ref, gain_ref, h_out, b_out, score, ctx):
+    tails = MAXB - 1
+    members = len(own_pieces)
+    stride = block_len // members
+
+    def body(*refs):
+        tail_refs, own_refs, refs = refs[:members], refs[members : 2 * members], refs[2 * members :]
+        q_ref, bias_ref, h_ref, gain_ref, wo_hbm, h_out, b_out = refs[:7]
+        score, ctx, wo_ref, kv_ref, arrived = refs[7:]
+        load = pltpu.make_async_copy(wo_hbm.at[layer], wo_ref, arrived)
+        load.start()
+        for member in range(members):
+            for slot in range(tails + blocks):
+                source = tail_refs[member] if slot < tails else own_refs[member]
+                at = (slot if slot < tails else slot - tails) * stride
+                to = slot * block_len + member * stride
+                kv_ref[to : to + stride] = source[at : at + stride]
         low = lax.broadcasted_iota(jnp.int32, (kv_ref.shape[0], LANES), 1) < HEAD_DIM
 
         def variants(x, other):
@@ -214,14 +233,15 @@
                 ctx[i * rows : (i + 1) * rows, j * LANES : (j + 1) * LANES] = jnp.where(
                     first, halves[(i, j, 0)], halves[(i, j, 1)]
                 )
+        load.wait()
         value = h_ref[...] + dot(ctx[...].astype(BF16), wo_ref[...])
         h_out[...] = value
         b_out[...] = norm_rows(value, gain_ref[...]).astype(BF16)
 
-    args = (q, kv, bias, h, w_out, gains)
+    args = [*tail_pieces, *own_pieces, q, bias, h, gains, in_hbm(w_out)]
     specs = [whole(x.shape) for x in args]
-    specs[4] = layer_of(w_out, layer)
-    specs[5] = layer_of(gains, layer)
+    specs[-2] = layer_of(gains, layer)
+    specs[-1] = pl.BlockSpec(memory_space=pl.ANY)
     outs = (
         jax.ShapeDtypeStruct((count, width), F32),
         jax.ShapeDtypeStruct((count, width), BF16),
@@ -235,6 +255,9 @@
         scratch_shapes=[
             pltpu.VMEM((blocks * heads * rows, span), F32),
             pltpu.VMEM((count, qw), F32),
+            pltpu.VMEM((qw, width), BF16),
+            pltpu.VMEM(((tails + blocks) * block_len, 2 * kvw), BF16),
+            pltpu.SemaphoreType.DMA,
         ],
         compiler_params=params(20),
         cost_estimate=cost(2.0 * count * width * width + 8.0 * count * qw * span, 0),
@@ -269,6 +292,57 @@
         cost_estimate=cost(6.0 * count * width * w_down.shape[1], 0),
         name="mlp",
     )(x, w_gate, w_up, w_down)
+
+
+def mlp_rows(rows, wg, wu, wd):
+    gate = dot_t(rows, wg[...])
+    upper = dot_t(rows, wu[...])
+    return dot((gate / (1.0 + jnp.exp(-gate)) * upper).astype(BF16), wd[...])
+
+
+def mlp_load(x, w_gate, w_up, w_down, layer):
+    stacks = (w_gate, w_up, w_down)
+
+    def body(x_ref, *refs):
+        sources, out_ref, kept, arrived = refs[:3], refs[3], refs[4:7], refs[7]
+        loads = [
+            pltpu.make_async_copy(source.at[layer], target, arrived.at[n])
+            for n, (source, target) in enumerate(zip(sources, kept))
+        ]
+        for load in loads:
+            load.start()
+        for load in loads:
+            load.wait()
+        out_ref[...] = mlp_rows(x_ref[...], *kept)
+
+    return pl.pallas_call(
+        body,
+        grid=(1,),
+        out_shape=[jax.ShapeDtypeStruct(x.shape, F32)]
+        + [pltpu.VMEM(w.shape[1:], BF16) for w in stacks],
+        in_specs=[whole(x.shape)] + [pl.BlockSpec(memory_space=pl.ANY)] * 3,
+        out_specs=[whole(x.shape)] + [pl.BlockSpec(memory_space=pltpu.VMEM)] * 3,
+        scratch_shapes=[pltpu.SemaphoreType.DMA((3,))],
+        compiler_params=params(12),
+        cost_estimate=cost(6.0 * x.size * w_down.shape[1], 0),
+        name="mlp_load",
+    )(x, *[in_hbm(w) for w in stacks])
+
+
+def mlp_kept(x, weights):
+    def body(x_ref, wg_ref, wu_ref, wd_ref, out_ref):
+        out_ref[...] = mlp_rows(x_ref[...], wg_ref, wu_ref, wd_ref).astype(BF16)
+
+    return pl.pallas_call(
+        body,
+        grid=(1,),
+        out_shape=jax.ShapeDtypeStruct(x.shape, BF16),
+        in_specs=[whole(x.shape)] + [pl.BlockSpec(memory_space=pltpu.VMEM)] * 3,
+        out_specs=whole(x.shape),
+        compiler_params=params(12),
+        cost_estimate=cost(6.0 * x.size * weights[2].shape[0], 0),
+        name="mlp_kept",
+    )(x, *[pltpu.with_memory_space_constraint(w, pltpu.VMEM) for w in weights])
 
 
 def last_norm(h, parts, gain):
@@ -367,7 +441,159 @@
         compiler_params=params(20),
         cost_estimate=cost(2.0 * count * width * cols * len(shards), 0),
         name="head_stats",
-    )(bases, wanted, *rows, *shards)
+    )(bases, wanted, *rows, *[in_hbm(w) for w in shards])
+
+
+def head_stats_mxu(rows, wanted, bases, shards):
+    count = sum(x.shape[0] for x in rows)
+    width = rows[0].shape[1]
+    cols = shards[0].shape[1]
+    deep, pair = 256, 512
+    tile = 2 * pair
+    per = cols // tile
+    steps = per * len(shards)
+    full, rest_k = width // deep, width % deep
+    starts = [k * deep for k in range(full)] + ([width - deep] if rest_k else [])
+    pieces = len(starts)
+    piece = count // pieces
+    padded = len(starts) * deep
+    cuts = 7 if width % 112 == 0 else 1
+
+    def body(base_ref, want_ref, *refs):
+        given = refs[: len(rows)]
+        sources = refs[len(rows) : len(rows) + len(shards)]
+        out_ref, top, total, picked, wide, x_ref, w_buf, arrived = refs[len(rows) + len(shards) :]
+        lane = lax.broadcasted_iota(jnp.int32, (1, LANES), 1)
+
+        def copy_part(source, at, slot, n):
+            part = pl.ds(n * (width // cuts), width // cuts)
+            return pltpu.make_async_copy(
+                source.at[part, pl.ds(at, tile)], w_buf.at[slot, part], arrived.at[slot, n]
+            )
+
+        def fetch(step):
+            for index, source in enumerate(sources):
+
+                @pl.when(step // per == index)
+                def _(source=source, index=index):
+                    at = pl.multiple_of((step - index * per) * tile, tile)
+                    for n in range(cuts):
+                        copy_part(source, at, step % 2, n).start()
+
+        def column(step):
+            start = base_ref[0] + step * tile
+            for index in range(1, len(shards)):
+                here = base_ref[index] + (step - index * per) * tile
+                start = jnp.where(step >= index * per, here, start)
+            return start
+
+        def scoped(*accs):
+            fetch(0)
+            top[...] = jnp.full_like(top, NEG)
+            total[...] = jnp.zeros_like(total)
+            picked[...] = jnp.zeros_like(picked)
+            wide[...] = jnp.broadcast_to(want_ref[...], wide.shape)
+            at = 0
+            for ref in given:
+                size = ref.shape[0]
+                x_ref[at : at + size, : full * deep] = ref[:, : full * deep]
+                if rest_k:
+                    blank = jnp.zeros((size, deep - rest_k), BF16)
+                    x_ref[at : at + size, full * deep : padded - rest_k] = blank
+                    x_ref[at : at + size, padded - rest_k :] = ref[:, full * deep :]
+                at += size
+            half = [[accs[(b * 2 + q) * pieces :][:pieces] for q in range(2)] for b in range(2)]
+
+            def multiply(b, slot, k):
+                for q in range(2):
+                    at = b * pair + q * deep
+                    register = k % 2
+                    pltpu.matmul_push_rhs(
+                        w_buf[slot, starts[k] : starts[k] + deep, at : at + deep],
+                        staging_register=register,
+                        mxu_index=q,
+                    )
+                    for n in range(pieces):
+                        pltpu.matmul_acc_lhs(
+                            half[b][q][n],
+                            x_ref[n * piece : (n + 1) * piece, k * deep : (k + 1) * deep],
+                            load_staged_rhs=register if n == 0 else None,
+                        )
+
+            def collect(b, n, start, fresh):
+                at = slice(n * piece, (n + 1) * piece)
+                parts = []
+                for q in range(2):
+                    found = pltpu.matmul_pop(half[b][q][n])
+                    parts += [found[:, c : c + LANES] for c in range(0, deep, LANES)]
+                best = parts[0]
+                for part in parts[1:]:
+                    best = jnp.maximum(best, part)
+                old = top[at]
+                best = jnp.maximum(best, old)
+                acc = total[at] * jnp.exp(old - best)
+                pick = picked[at]
+                local = wide[at]
+                for c, part in enumerate(parts):
+                    acc = acc + jnp.exp(part - best)
+                    pick = pick + jnp.where(local == lane + (start + c * LANES), part, 0.0)
+                if fresh is not None:
+                    best = jnp.where(fresh, NEG, best)
+                    acc = jnp.where(fresh, 0.0, acc)
+                    pick = jnp.where(fresh, 0.0, pick)
+                top[at] = best
+                total[at] = acc
+                picked[at] = pick
+
+            def step_fn(step, carry):
+                slot = step % 2
+                for n in range(cuts):
+                    copy_part(sources[0], 0, slot, n).wait()
+                pl.when(step + 1 < steps)(lambda: fetch(step + 1))
+                before = column(jnp.maximum(step - 1, 0)) + pair
+                start = column(step)
+                for k in range(len(starts)):
+                    multiply(0, slot, k)
+                    collect(1, k, before, step == 0)
+                for k in range(len(starts)):
+                    multiply(1, slot, k)
+                    collect(0, k, start, None)
+                return carry
+
+            lax.fori_loop(0, steps, step_fn, 0)
+            for k in range(pieces):
+                collect(1, k, column(steps - 1) + pair, None)
+            best = jnp.max(top[...], axis=1, keepdims=True)
+            acc = jnp.sum(total[...] * jnp.exp(top[...] - best), axis=1, keepdims=True)
+            pick = jnp.sum(picked[...], axis=1, keepdims=True)
+            packed = jnp.where(lane == 0, best, jnp.where(lane == 1, acc, pick))
+            out_ref[...] = jnp.transpose(packed, (1, 0))[:8]
+
+        kinds = [pltpu.ACC(q)((piece, deep), F32) for b in range(2) for q in range(2) for n in range(pieces)]
+        pl.run_scoped(scoped, *kinds)
+
+    return pl.pallas_call(
+        body,
+        grid=(1,),
+        out_shape=jax.ShapeDtypeStruct((8, count), F32),
+        in_specs=[
+            pl.BlockSpec(memory_space=pltpu.SMEM),
+            whole(wanted.shape),
+        ]
+        + [whole(x.shape) for x in rows]
+        + [pl.BlockSpec(memory_space=pl.ANY)] * len(shards),
+        out_specs=whole((8, count)),
+        scratch_shapes=[pltpu.VMEM((count, LANES), F32)] * 3
+        + [
+            pltpu.VMEM((count, LANES), jnp.int32),
+            pltpu.VMEM((count, padded), BF16),
+            pltpu.VMEM((2, width, tile), BF16),
+            pltpu.SemaphoreType.DMA((2, cuts)),
+        ],
+        compiler_params=params(20),
+        cost_estimate=cost(2.0 * count * width * cols * len(shards), 0),
+        name="head_stats_mxu",
+    )(bases, wanted, *rows, *[in_hbm(w) for w in shards])
 
 
 def shift(x, axes, distance, size, wrap):
@@ -422,7 +648,7 @@
     bases = jnp.stack([(r * tp_count + column) * vocab_shard for r in holders]).astype(jnp.int32)
     ids = targets.reshape(1, own_count)
     digits = jnp.concatenate([ids // 16384, ids // 128 % 128, ids % 128], axis=0).astype(BF16)
-    digits = jnp.pad(digits, ((0, slice_len - 3), (0, 4 * HEAD_DIM - own_count)))[None]
+    digits = jnp.pad(digits, ((0, slice_len - 3), (0, 2 * w_key.shape[-1] - own_count)))
 
     owner, offset = doc_table(doc_blocks, nblk)
     own_ids = row * own_blocks + jnp.arange(own_blocks, dtype=jnp.int32)
@@ -461,15 +687,18 @@
         kv = kv.reshape(own_blocks, slice_len, kvw)
         tail = shift(kv[own_blocks - tails :], DP, 1, dp_count, False)
         q = queries(a, w_query, cosine, sine, layer)
-        kv = jnp.concatenate([tail, kv] + ([digits] if layer == 0 else []), axis=0)
+        kv = jnp.concatenate([tail, kv] + ([digits[None]] if layer == 0 else []), axis=0)
         kv = lax.all_gather(kv, "tensor", axis=1, tiled=True)
         if layer == 0:
             found = kv[-1].reshape(tp_count, slice_len, kvw)[:, :3, :own_count].astype(jnp.int32)
             wanted_row = found[:, 0] * 16384 + found[:, 1] * 128 + found[:, 2]
             kv = kv[:-1]
+        tail_pieces = [kv[:tails].reshape(-1, kvw)]
+        own_pieces = [kv[tails:].reshape(-1, kvw)]
         h, b = attention(
             q,
-            kv.reshape(-1, kvw),
+            tail_pieces,
+            own_pieces,
             bias,
             h,
             w_out,
@@ -477,10 +706,11 @@
             layer,
         )
         if direct:
-            given = [b] + [peer(b, k) for k in range(1, tp_count)]
-            kinds = [F32] + [BF16] * (tp_count - 1)
-            parts = [mlp(x, w_gate, w_up, w_down, layer, t) for x, t in zip(given, kinds)]
-            parts = parts[:1] + [peer(parts[k], k) for k in range(1, tp_count)]
+            given = [peer(b, k) for k in range(1, tp_count)]
+            mine, *kept = mlp_load(b, w_gate, w_up, w_down, layer)
+            parts = [mine]
+            for k, x in enumerate(given, 1):
+                parts.append(peer(mlp_kept(x, kept), k))
         else:
             flat = lax.all_gather(b, "tensor", axis=0, tiled=True)
             out = mlp(flat, w_gate, w_up, w_down, layer, BF16)
@@ -490,47 +720,54 @@
     final = last_norm(h, parts, tall(final_gain))
 
     zq_count = lax.axis_size("zq")
-    pieces = []
-    for turn_q in range(zq_count):
-        for turn in range(zp_count):
-            rows, wanted = final, wanted_row
-            if turn:
-                rows = shift(rows, "zp", turn, zp_count, True)
-                wanted = shift(wanted, "zp", turn, zp_count, True)
-            if turn_q:
-                rows = shift(rows, "zq", turn_q, zq_count, True)
-                wanted = shift(wanted, "zq", turn_q, zq_count, True)
-            pieces.append((rows, wanted))
+    turns = [(q, p) for q in range(zq_count) for p in range(zp_count)]
+
+    def brought(x, turn):
+        if turn == (0, 0):
+            return x
+        route = [
+            (p * zq_count + q, (p + turn[1]) % zp_count * zq_count + (q + turn[0]) % zq_count)
+            for p in range(zp_count)
+            for q in range(zq_count)
+        ]
+        return lax.ppermute(x, ("zp", "zq"), route)
+
+    def gathered(x):
+        if direct:
+            return [x] + [peer(x, k) for k in range(1, tp_count)]
+        return [lax.all_gather(x, "tensor", axis=0, tiled=True)]
+
+    if direct:
+        order = [column ^ k for k in range(tp_count)]
+        wanted_row = [lax.dynamic_slice_in_dim(wanted_row, k, 1, 0) for k in order]
+        wanted_row = jnp.concatenate(wanted_row)
+    wanted = [brought(wanted_row, turn).reshape(-1, 1) for turn in turns]
+    chunk = gathered(final)
+    done = chunk[-1]
+    queue = [brought(final, turn) for turn in turns[1:3]]
     stats = []
-    first = lax.all_gather(final, "tensor", axis=0, tiled=True)
-    chunk, done = [first], first
-    order = [column ^ k for k in range(tp_count)]
-    for n in range(len(pieces)):
-        wanted = pieces[n][1]
-        if n and direct:
-            wanted = [lax.dynamic_slice_in_dim(wanted, k, 1, 0) for k in order]
-            wanted = jnp.concatenate(wanted, axis=0)
+    for n in range(len(turns)):
         following = None
-        if n + 1 < len(pieces):
-            rows, done = lax.optimization_barrier((pieces[n + 1][0], done))
-            if direct:
-                following = [rows] + [peer(rows, k) for k in range(1, tp_count)]
-            else:
-                following = [lax.all_gather(rows, "tensor", axis=0, tiled=True)]
-        stats.append(head_stats(chunk, wanted.reshape(-1, 1), bases, shards))
-        chunk, done = following, stats[-1]
-    stats = jnp.stack(stats)
-    stats = stats.reshape(zq_count, zp_count, 8, tp_count, own_count)
-    if direct:
-        mixed = [jnp.take(stats, column ^ jnp.arange(tp_count), axis=3)]
-        plain = stats.reshape(-1, 8, tp_count, own_count)[:1]
-        mixed = mixed[0].reshape(-1, 8, tp_count, own_count)[1:]
-        stats = jnp.concatenate([plain, mixed]).reshape(stats.shape)
-    zp_at = (lax.axis_index("zp") - jnp.arange(zp_count)) % zp_count
-    zq_at = (lax.axis_index("zq") - jnp.arange(zq_count)) % zq_count
-    stats = jnp.take(jnp.take(stats, zp_at, axis=1), zq_at, axis=0)
-    stats = stats[:, :, :3].transpose(1, 0, 3, 2, 4)
-    stats = stats.reshape(zp_count * zq_count * tp_count, 3, own_count)
+        if n + 1 < len(turns):
+            ahead, source, done = lax.optimization_barrier((queue.pop(0), final, done))
+            following = gathered(ahead)
+            if n + 3 < len(turns):
+                queue.append(brought(source, turns[n + 3]))
+        fits = vocab_shard % 1024 == 0 and sum(x.shape[0] for x in chunk) % 64 == 0
+        stage = head_stats_mxu if fits else head_stats
+        stats.append(stage(chunk, wanted[n], bases, shards))
+        chunk = following
+        bases, done = lax.optimization_barrier((bases, stats[-1]))
+        stats[-1] = done
+    stats = jnp.stack(stats)[:, :3].reshape(len(turns), 3, tp_count, own_count)
+    stats = stats.transpose(0, 2, 1, 3).reshape(-1, 3, own_count)
+    place_zp = jnp.arange(zp_count)[:, None, None]
+    place_zq = jnp.arange(zq_count)[None, :, None]
+    place_t = jnp.arange(tp_count)[None, None, :]
+    at = (lax.axis_index("zq") - place_zq) % zq_count * zp_count
+    at = (at + (lax.axis_index("zp") - place_zp) % zp_count) * tp_count
+    at = at + (place_t ^ column if direct else place_t)
+    stats = jnp.take(stats, at.reshape(-1), axis=0, mode="clip")
     stats = lax.all_to_all(stats, ("zp", "zq", "tensor"), 0, 0, tiled=False)
     peak = jnp.max(stats[:, 0], axis=0)
     total = jnp.sum(stats[:, 1] * jnp.exp(stats[:, 0] - peak[None]), axis=0)

time: 231 us -> 203 us (0.88)
  local copies, waits for them, and re-layouts: 40 us -> 5.59 us
  blocking collectives: 43.7 us -> 29.2 us
  waiting for transfers between devices: 18.1 us -> 29.1 us
  Pallas kernels: 76 us -> 84.4 us
  starting transfers between devices: 44.3 us -> 49.8 us
  other arithmetic: 6.5 us -> 3.26 us
    unnamed x92 -> x14, local copies, waits for them, and re-layouts: 32.7 us -> 1.05 us
    all_gather x1 -> x0, blocking collectives: 14 us -> none  [on_device(): first = lax.all_gather(final, 'tensor', axis=0, tiled=True)]
    ppermute x0 -> x6, starting transfers between devices: none -> 10.5 us  [brought(): return lax.ppermute(x, ('zp', 'zq'), route)]
    ppermute x8 -> x2, starting transfers between devices: 11.6 us -> 3.69 us  [shift(): return lax.ppermute(x, axes, pairs)]
    ppermute x0 -> x6, waiting for transfers between devices: none -> 6.99 us  [brought(): return lax.ppermute(x, ('zp', 'zq'), route)]
    ppermute x21 -> x24, waiting for transfers between devices: 10.7 us -> 14.7 us  [peer(): return lax.ppermute(x, 'tensor', [(i, i ^ k) for i in range(tp_count)])]
    ppermute x21 -> x24, starting transfers between devices: 25.1 us -> 28.7 us  [peer(): return lax.ppermute(x, 'tensor', [(i, i ^ k) for i in range(tp_count)])]
    pallas_call x2, Pallas kernels: 1.17 us -> 4.02 us  [queries(): pl.pallas_call(body, grid=(1,), out_shape=jax.ShapeDtypeStruct(shape, BF1...]
  transfers between devices with their start and end apart: 31 -> 34, of which waited for: 4 -> 8; matrix products, arithmetic and copies ran while one was open for 3% -> 1% of each run, Pallas kernels for 27% -> 35%
where the time goes in v2:
time: 203 us
  Pallas kernels  84.4 us (42%)
  starting transfers between devices  49.8 us (25%)
  blocking collectives  29.2 us (14%)
  waiting for transfers between devices  29.1 us (14%)
  local copies, waits for them, and re-layouts  5.59 us (3%)
  other arithmetic  3.26 us (2%)
    pallas_call x4, Pallas kernels, head_stats_mxu(): pl.pallas_call(body, grid=(1,), out_shape=jax.ShapeDtypeStruct((8, count)...  50 us
    ppermute x24, starting transfers between devices, peer(): return lax.ppermute(x, 'tensor', [(i, i ^ k) for i in range(tp_count)])  28.7 us
    all_gather x2, blocking collectives, on_device(): kv = lax.all_gather(kv, 'tensor', axis=1, tiled=True)  20.3 us
    ppermute x24, waiting for transfers between devices, peer(): return lax.ppermute(x, 'tensor', [(i, i ^ k) for i in range(tp_count)])  14.7 us
    pallas_call x6, Pallas kernels, mlp_kept(): pl.pallas_call(body, grid=(1,), out_shape=jax.ShapeDtypeStruct(x.shape, B...  10.9 us
    ppermute x6, starting transfers between devices, brought(): return lax.ppermute(x, ('zp', 'zq'), route)  10.5 us
    pallas_call x2, Pallas kernels, mlp_load(): pl.pallas_call(body, grid=(1,), out_shape=[jax.ShapeDtypeStruct(x.shape,...  9.55 us
    all_to_all x1, blocking collectives, on_device(): lax.all_to_all(spread, ALL, 0, 0, tiled=False)  8.9 us
  transfers between devices with their start and end apart: 34, of which 8 were waited for; matrix products, arithmetic and copies ran while one was open for 1% of the time, Pallas kernels for 35%

profile of v2, /device:TPU:0, one launch (start us, length us, event | category | flops | bytes accessed | tf_op | source)
XLA Modules:
  0.0 202.6 jit_solution(16340554525623454925)
XLA Ops:
  6.2 2.4 %collective-permute-start = (bf16[3,32,256]{2,1,0:T(8,128)(2,1)S(1)}, bf16[3,32,256]{2,1,0:T(8,128)(2,1)S(1)}, u32[]{:S(2)}, u32[]{:S(2)}) collective-permute-start(bf16[3,32,256]{2,1,0:T(8,128)(2,1)S(1)} %bitcast.73), channel_id=1, source_target_pairs={{0,4},{4,8},{8,12},{12,16},{16,20},{20,24},{24,28},{1,5},{5,9},{9,... | collective-permute-start | bytes 147464 | tf_op jit(solution)/shard_map/ppermute | solution.py:601
  8.6 2.7 %collective-permute-start.17 = (bf16[896,3072]{1,0:T(8,128)(2,1)}, bf16[896,3072]{1,0:T(8,128)(2,1)}, u32[]{:S(2)}, u32[]{:S(2)}) collective-permute-start(bf16[896,3072]{1,0:T(8,128)(2,1)} %refs_4_.7), channel_id=1, source_target_pairs={{0,4},{4,0},{1,5},{5,1},{2,6},{6,2},{3,7},{7,3},{8,12},{12,8},{9,1... | collective-permute-start | bytes 16515080 | tf_op jit(solution)/shard_map/ppermute | solution.py:643
  12.9 2.0 queries.2.refs_2_
  15.0 10.0 %all_gather.6 = bf16[8,128,256]{2,1,0:T(8,128)(2,1)S(1)} all-gather(bf16[8,32,256]{2,1,0:T(8,128)(2,1)S(1)} %pad_maximum_fusion), channel_id=1, replica_groups=mesh['zp'=2,'zq'=2,'core'=2,'tensor'=4] {'tensor'}, dimensions={1}, use_global_device_ids=true | all-gather | bytes 655360 | tf_op jit(solution)/shard_map/all_gather | solution.py:691
  25.1 3.1 %attention.2 = (f32[128,896]{1,0:T(8,128)S(1)}, bf16[128,896]{1,0:T(8,128)(2,1)S(1)}) custom-call(bf16[384,256]{1,0:T(8,128)(2,1)S(1)} %bitcast.58, bf16[512,256]{1,0:T(8,128)(2,1)S(1)} %bitcast.56, bf16[128,896]{1,0:T(8,128)(2,1)S(1)} %queries.2.refs_2_, f32[4,32,512]{2,1,0:T(8,128)S(1)} %and_select_fusion.refs_3_, ...), custom_call_target="tpu_custom_call" | custom-call | flops 675282944 | tf_op jit(solution)/shard_map/attention/pallas_call | solution.py:249
  31.8 4.8 %mlp_load.2 = (f32[128,896]{1,0:T(8,128)S(1)}, bf16[1216,896]{1,0:T(8,128)(2,1)S(1)}, bf16[1216,896]{1,0:T(8,128)(2,1)S(1)}, bf16[1216,896]{1,0:T(8,128)(2,1)S(1)}) custom-call(bf16[128,896]{1,0:T(8,128)(2,1)S(1)} %get-tuple-element.35.x_ref, bf16[2,1216,896]{2,1,0:T(8,128)(2,1)} %bitcast.66, bf16[2,1216,896]{2,1,0:T(8,128)(2,1)} %bitcast.68, ...), custom_call_target="tpu_custom_call" | custom-call | flops 836763648 | tf_op jit(solution)/shard_map/mlp_load/pallas_call | solution.py:318
  36.6 1.8 mlp_kept.6
  40.0 1.8 mlp_kept.7
  42.4 1.8 mlp_kept.8
  45.9 6.4 %collective-permute-done.4.refs_3_ = bf16[128,896]{1,0:T(8,128)(2,1)S(1)} collective-permute-done((bf16[128,896]{1,0:T(8,128)(2,1)S(1)}, bf16[128,896]{1,0:T(8,128)(2,1)S(1)}, u32[]{:S(2)}, u32[]{:S(2)}) %collective-permute-start.4) | collective-permute-done | bytes 229408 | tf_op jit(solution)/shard_map/ppermute | solution.py:639
  55.1 2.0 queries.3.refs_2_
  57.2 10.2 %all_gather.7 = bf16[7,128,256]{2,1,0:T(8,128)(2,1)S(1)} all-gather(bf16[7,32,256]{2,1,0:T(8,128)(2,1)S(1)} %pad_maximum_fusion.1), channel_id=1, replica_groups=mesh['zp'=2,'zq'=2,'core'=2,'tensor'=4] {'tensor'}, dimensions={1}, use_global_device_ids=true | all-gather | bytes 573440 | tf_op jit(solution)/shard_map/all_gather | solution.py:691
  67.4 3.7 %attention.3 = (f32[128,896]{1,0:T(8,128)S(1)}, bf16[128,896]{1,0:T(8,128)(2,1)S(1)}) custom-call(bf16[384,256]{1,0:T(8,128)(2,1)S(1)} %bitcast.57, bf16[512,256]{1,0:T(8,128)(2,1)S(1)} %bitcast.55, bf16[128,896]{1,0:T(8,128)(2,1)S(1)} %queries.3.refs_2_, f32[4,32,512]{2,1,0:T(8,128)S(1)} %and_select_fusion.refs_3_, ...), custom_call_target="tpu_custom_call" | custom-call | flops 675282944 | tf_op jit(solution)/shard_map/attention/pallas_call | solution.py:249
  74.7 4.8 %mlp_load.3 = (f32[128,896]{1,0:T(8,128)S(1)}, bf16[1216,896]{1,0:T(8,128)(2,1)S(1)}, bf16[1216,896]{1,0:T(8,128)(2,1)S(1)}, bf16[1216,896]{1,0:T(8,128)(2,1)S(1)}) custom-call(bf16[128,896]{1,0:T(8,128)(2,1)S(1)} %get-tuple-element.44.x_ref, bf16[2,1216,896]{2,1,0:T(8,128)(2,1)} %bitcast.67, bf16[2,1216,896]{2,1,0:T(8,128)(2,1)} %bitcast.69, ...), custom_call_target="tpu_custom_call" | custom-call | flops 836763648 | tf_op jit(solution)/shard_map/mlp_load/pallas_call | solution.py:318
  79.7 1.8 mlp_kept.9
  82.6 1.8 collective-permute-done.10.x_ref
  84.4 1.8 mlp_kept.10
  87.3 1.8 mlp_kept.11
  90.7 2.0 collective-permute-start.18
  94.2 3.4 %collective-permute-done.11.refs_2_ = bf16[128,896]{1,0:T(8,128)(2,1)S(1)} collective-permute-done((bf16[128,896]{1,0:T(8,128)(2,1)S(1)}, bf16[128,896]{1,0:T(8,128)(2,1)S(1)}, u32[]{:S(2)}, u32[]{:S(2)}) %collective-permute-start.11) | collective-permute-done | bytes 229408 | tf_op jit(solution)/shard_map/ppermute | solution.py:639
  101.5 1.6 collective-permute-done.28
  104.9 2.9 %collective-permute-done.16.refs_3_ = bf16[128,896]{1,0:T(8,128)(2,1)S(1)} collective-permute-done((bf16[128,896]{1,0:T(8,128)(2,1)S(1)}, bf16[128,896]{1,0:T(8,128)(2,1)S(1)}, u32[]{:S(2)}, u32[]{:S(2)}) %collective-permute-start.16) | collective-permute-done | bytes 229408 | tf_op jit(solution)/shard_map/ppermute | solution.py:639
  107.7 4.2 %collective-permute-start.24 = (bf16[128,896]{1,0:T(8,128)(2,1)S(1)}, bf16[128,896]{1,0:T(8,128)(2,1)S(1)}, u32[]{:S(2)}, u32[]{:S(2)}) collective-permute-start(bf16[128,896]{1,0:T(8,128)(2,1)S(1)} %last_norm.1.refs_0_), channel_id=1, source_target_pairs={{0,8},{8,0},{16,24},{24,16},{1,9},{9,1},{17,25},{25,17},{2,10},{10... | collective-permute-start | bytes 688136 | tf_op jit(solution)/shard_map/ppermute | solution.py:733
  111.9 5.3 %collective-permute-done.19.refs_0_ = bf16[128,896]{1,0:T(8,128)(2,1)S(1)} collective-permute-done((bf16[128,896]{1,0:T(8,128)(2,1)S(1)}, bf16[128,896]{1,0:T(8,128)(2,1)S(1)}, u32[]{:S(2)}, u32[]{:S(2)}) %collective-permute-start.19) | collective-permute-done | bytes 229408 | tf_op jit(solution)/shard_map/ppermute | solution.py:733
  120.8 1.9 collective-permute-start.29
  122.6 12.5 %head_stats_mxu.4 = f32[8,512]{1,0:T(8,128)S(1)} custom-call(s32[2]{0:T(128)S(1)} %pad_add_fusion.2.base_ref, s32[512,1]{1,0:T(8,128)S(1)} %copy.32.want_ref, bf16[128,896]{1,0:T(8,128)(2,1)S(1)} %last_norm.1.refs_0_, bf16[128,896]{1,0:T(8,128)(2,1)S(1)} %collective-permute-done.14.refs_1_, bf16[128,896]{1,0:T(8,128)(2,1)S(1)} %collective-permute-done.15.refs_2_, ...), custom_call_target="tpu_custom_call" | custom-call | flops 5637144576 | tf_op jit(solution)/shard_map/head_stats_mxu/pallas_call | solution.py:575
  138.7 12.5 %head_stats_mxu.5 = f32[8,512]{1,0:T(8,128)S(1)} custom-call(s32[2]{0:T(128)S(1)} %pad_add_fusion.2.base_ref, s32[512,1]{1,0:T(8,128)S(1)} %copy.33.want_ref, bf16[128,896]{1,0:T(8,128)(2,1)S(1)} %collective-permute-done.19.refs_0_, bf16[128,896]{1,0:T(8,128)(2,1)S(1)} %collective-permute-done.20.refs_1_, ...), custom_call_target="tpu_custom_call" | custom-call | flops 5637144576 | tf_op jit(solution)/shard_map/head_stats_mxu/pallas_call | solution.py:575
  154.8 12.5 %head_stats_mxu.6 = f32[8,512]{1,0:T(8,128)S(1)} custom-call(s32[2]{0:T(128)S(1)} %pad_add_fusion.2.base_ref, s32[512,1]{1,0:T(8,128)S(1)} %copy.34.want_ref, bf16[128,896]{1,0:T(8,128)(2,1)S(1)} %collective-permute-done.24.refs_0_, bf16[128,896]{1,0:T(8,128)(2,1)S(1)} %collective-permute-done.25.refs_1_, ...), custom_call_target="tpu_custom_call" | custom-call | flops 5637144576 | tf_op jit(solution)/shard_map/head_stats_mxu/pallas_call | solution.py:575
  167.4 12.5 %head_stats_mxu.7 = f32[8,512]{1,0:T(8,128)S(1)} custom-call(s32[2]{0:T(128)S(1)} %pad_add_fusion.2.base_ref, s32[512,1]{1,0:T(8,128)S(1)} %copy.35.want_ref, bf16[128,896]{1,0:T(8,128)(2,1)S(1)} %collective-permute-done.29.refs_0_, bf16[128,896]{1,0:T(8,128)(2,1)S(1)} %collective-permute-done.30.refs_1_, ...), custom_call_target="tpu_custom_call" | custom-call | flops 5637144576 | tf_op jit(solution)/shard_map/head_stats_mxu/pallas_call | solution.py:575
  181.1 4.2 %all-to-all-start = ((f32[16,3,128]{2,1,0:T(4,128)}), f32[16,3,128]{2,1,0:T(4,128)S(1)}, u32[]{:S(2)}, u32[]{:S(2)}) async-start(f32[16,3,128]{2,1,0:T(4,128)} %gather_fusion), calls=%async_computation | async-start | bytes 65536 | tf_op jit(solution)/shard_map/all_to_all | solution.py:771
  185.3 7.4 %all-to-all-done = f32[16,3,128]{2,1,0:T(4,128)S(1)} async-done(((f32[16,3,128]{2,1,0:T(4,128)}), f32[16,3,128]{2,1,0:T(4,128)S(1)}, u32[]{:S(2)}, u32[]{:S(2)}) %all-to-all-start) | async-done | bytes 24608 | tf_op jit(solution)/shard_map/all_to_all | solution.py:771
  193.1 8.9 %all_to_all.11 = f32[32,1,128]{2,1,0:T(1,128)S(1)} all-to-all(f32[32,1,128]{2,1,0:T(1,128)S(1)} %broadcast_in_dim.152), channel_id=1, replica_groups=mesh['zp'=2,'zq'=2,'core'=2,'tensor'=4] {'zp','zq','core','tensor'}, dimensions={0} | all-to-all | bytes 32768 | tf_op jit(solution)/shard_map/all_to_all | solution.py:782
  (144 shorter events, 44.6 us)
Async XLA Ops:
  6.2 8.7 %collective-permute-start = (bf16[3,32,256]{2,1,0:T(8,128)(2,1)S(1)}, bf16[3,32,256]{2,1,0:T(8,128)(2,1)S(1)}, u32[]{:S(2)}, u32[]{:S(2)}) collective-permute-start(bf16[3,32,256]{2,1,0:T(8,128)(2,1)S(1)} %bitcast.73), channel_id=1, source_target_pairs={{0,4},{4,8},{8,12},{12,16},{16,20},{20,24},{24,28},{1,5},{5,9},{9,... | collective-permute-start | bytes 147464 | tf_op jit(solution)/shard_map/ppermute | solution.py:601
  8.6 112.2 %collective-permute-start.17 = (bf16[896,3072]{1,0:T(8,128)(2,1)}, bf16[896,3072]{1,0:T(8,128)(2,1)}, u32[]{:S(2)}, u32[]{:S(2)}) collective-permute-start(bf16[896,3072]{1,0:T(8,128)(2,1)} %refs_4_.7), channel_id=1, source_target_pairs={{0,4},{4,0},{1,5},{5,1},{2,6},{6,2},{3,7},{7,3},{8,12},{12,8},{9,1... | collective-permute-start | bytes 16515080 | tf_op jit(solution)/shard_map/ppermute | solution.py:643
  28.2 8.3 %collective-permute-start.1 = (bf16[128,896]{1,0:T(8,128)(2,1)S(1)}, bf16[128,896]{1,0:T(8,128)(2,1)S(1)}, u32[]{:S(2)}, u32[]{:S(2)}) collective-permute-start(bf16[128,896]{1,0:T(8,128)(2,1)S(1)} %get-tuple-element.35.x_ref), channel_id=1, source_target_pairs={{0,1},{1,0},{2,3},{3,2},{4,5},{5,4},{6,7},{7,6},{8,9},{9,8},{10,11... | collective-permute-start | bytes 688136 | tf_op jit(solution)/shard_map/ppermute | solution.py:639
  29.8 10.2 %collective-permute-start.3 = (bf16[128,896]{1,0:T(8,128)(2,1)S(1)}, bf16[128,896]{1,0:T(8,128)(2,1)S(1)}, u32[]{:S(2)}, u32[]{:S(2)}) collective-permute-start(bf16[128,896]{1,0:T(8,128)(2,1)S(1)} %get-tuple-element.35.x_ref), channel_id=1, source_target_pairs={{0,2},{1,3},{2,0},{3,1},{4,6},{5,7},{6,4},{7,5},{8,10},{9,11},{10,... | collective-permute-start | bytes 688136 | tf_op jit(solution)/shard_map/ppermute | solution.py:639
  30.3 12.0 %collective-permute-start.5 = (bf16[128,896]{1,0:T(8,128)(2,1)S(1)}, bf16[128,896]{1,0:T(8,128)(2,1)S(1)}, u32[]{:S(2)}, u32[]{:S(2)}) collective-permute-start(bf16[128,896]{1,0:T(8,128)(2,1)S(1)} %get-tuple-element.35.x_ref), channel_id=1, source_target_pairs={{0,3},{1,2},{2,1},{3,0},{4,7},{5,6},{6,5},{7,4},{8,11},{9,10},{10,... | collective-permute-start | bytes 688136 | tf_op jit(solution)/shard_map/ppermute | solution.py:639
  38.4 7.5 %collective-permute-start.2 = (bf16[128,896]{1,0:T(8,128)(2,1)S(1)}, bf16[128,896]{1,0:T(8,128)(2,1)S(1)}, u32[]{:S(2)}, u32[]{:S(2)}) collective-permute-start(bf16[128,896]{1,0:T(8,128)(2,1)S(1)} %mlp_kept.6), channel_id=1, source_target_pairs={{0,1},{1,0},{2,3},{3,2},{4,5},{5,4},{6,7},{7,6},{8,9},{9,8},{10,11... | collective-permute-start | bytes 688136 | tf_op jit(solution)/shard_map/ppermute | solution.py:639
  41.8 10.5 %collective-permute-start.4 = (bf16[128,896]{1,0:T(8,128)(2,1)S(1)}, bf16[128,896]{1,0:T(8,128)(2,1)S(1)}, u32[]{:S(2)}, u32[]{:S(2)}) collective-permute-start(bf16[128,896]{1,0:T(8,128)(2,1)S(1)} %mlp_kept.7), channel_id=1, source_target_pairs={{0,2},{1,3},{2,0},{3,1},{4,6},{5,7},{6,4},{7,5},{8,10},{9,11},{10,... | collective-permute-start | bytes 688136 | tf_op jit(solution)/shard_map/ppermute | solution.py:639
  44.2 8.0 %collective-permute-start.6 = (bf16[128,896]{1,0:T(8,128)(2,1)S(1)}, bf16[128,896]{1,0:T(8,128)(2,1)S(1)}, u32[]{:S(2)}, u32[]{:S(2)}) collective-permute-start(bf16[128,896]{1,0:T(8,128)(2,1)S(1)} %mlp_kept.8), channel_id=1, source_target_pairs={{0,3},{1,2},{2,1},{3,0},{4,7},{5,6},{6,5},{7,4},{8,11},{9,10},{10,... | collective-permute-start | bytes 688136 | tf_op jit(solution)/shard_map/ppermute | solution.py:639
  71.1 8.5 %collective-permute-start.8 = (bf16[128,896]{1,0:T(8,128)(2,1)S(1)}, bf16[128,896]{1,0:T(8,128)(2,1)S(1)}, u32[]{:S(2)}, u32[]{:S(2)}) collective-permute-start(bf16[128,896]{1,0:T(8,128)(2,1)S(1)} %get-tuple-element.44.x_ref), channel_id=1, source_target_pairs={{0,1},{1,0},{2,3},{3,2},{4,5},{5,4},{6,7},{7,6},{8,9},{9,8},{10,11... | collective-permute-start | bytes 688136 | tf_op jit(solution)/shard_map/ppermute | solution.py:639
  72.2 12.2 %collective-permute-start.10 = (bf16[128,896]{1,0:T(8,128)(2,1)S(1)}, bf16[128,896]{1,0:T(8,128)(2,1)S(1)}, u32[]{:S(2)}, u32[]{:S(2)}) collective-permute-start(bf16[128,896]{1,0:T(8,128)(2,1)S(1)} %get-tuple-element.44.x_ref), channel_id=1, source_target_pairs={{0,2},{1,3},{2,0},{3,1},{4,6},{5,7},{6,4},{7,5},{8,10},{9,11},{10,... | collective-permute-start | bytes 688136 | tf_op jit(solution)/shard_map/ppermute | solution.py:639
  73.2 14.1 %collective-permute-start.12 = (bf16[128,896]{1,0:T(8,128)(2,1)S(1)}, bf16[128,896]{1,0:T(8,128)(2,1)S(1)}, u32[]{:S(2)}, u32[]{:S(2)}) collective-permute-start(bf16[128,896]{1,0:T(8,128)(2,1)S(1)} %get-tuple-element.44.x_ref), channel_id=1, source_target_pairs={{0,3},{1,2},{2,1},{3,0},{4,7},{5,6},{6,5},{7,4},{8,11},{9,10},{10,... | collective-permute-start | bytes 688136 | tf_op jit(solution)/shard_map/ppermute | solution.py:639
  81.5 11.2 %collective-permute-start.9 = (bf16[128,896]{1,0:T(8,128)(2,1)S(1)}, bf16[128,896]{1,0:T(8,128)(2,1)S(1)}, u32[]{:S(2)}, u32[]{:S(2)}) collective-permute-start(bf16[128,896]{1,0:T(8,128)(2,1)S(1)} %mlp_kept.9), channel_id=1, source_target_pairs={{0,1},{1,0},{2,3},{3,2},{4,5},{5,4},{6,7},{7,6},{8,9},{9,8},{10,11... | collective-permute-start | bytes 688136 | tf_op jit(solution)/shard_map/ppermute | solution.py:639
  86.2 11.4 %collective-permute-start.11 = (bf16[128,896]{1,0:T(8,128)(2,1)S(1)}, bf16[128,896]{1,0:T(8,128)(2,1)S(1)}, u32[]{:S(2)}, u32[]{:S(2)}) collective-permute-start(bf16[128,896]{1,0:T(8,128)(2,1)S(1)} %mlp_kept.10), channel_id=1, source_target_pairs={{0,2},{1,3},{2,0},{3,1},{4,6},{5,7},{6,4},{7,5},{8,10},{9,11},{10,... | collective-permute-start | bytes 688136 | tf_op jit(solution)/shard_map/ppermute | solution.py:639
  89.1 8.6 %collective-permute-start.13 = (bf16[128,896]{1,0:T(8,128)(2,1)S(1)}, bf16[128,896]{1,0:T(8,128)(2,1)S(1)}, u32[]{:S(2)}, u32[]{:S(2)}) collective-permute-start(bf16[128,896]{1,0:T(8,128)(2,1)S(1)} %mlp_kept.11), channel_id=1, source_target_pairs={{0,3},{1,2},{2,1},{3,0},{4,7},{5,6},{6,5},{7,4},{8,11},{9,10},{10,... | collective-permute-start | bytes 688136 | tf_op jit(solution)/shard_map/ppermute | solution.py:639
  90.7 8.3 %collective-permute-start.18 = (s32[4,128]{1,0:T(4,128)S(1)}, s32[4,128]{1,0:T(4,128)S(1)}, u32[]{:S(2)}, u32[]{:S(2)}) collective-permute-start(s32[4,128]{1,0:T(4,128)S(1)} %pad_add_fusion), channel_id=1, source_target_pairs={{0,16},{8,24},{16,0},{24,8},{1,17},{9,25},{17,1},{25,9},{2,18},{10... | collective-permute-start | bytes 6152 | tf_op jit(solution)/shard_map/ppermute | solution.py:733
  92.7 7.4 %collective-permute-start.23 = (s32[4,128]{1,0:T(4,128)S(1)}, s32[4,128]{1,0:T(4,128)S(1)}, u32[]{:S(2)}, u32[]{:S(2)}) collective-permute-start(s32[4,128]{1,0:T(4,128)S(1)} %pad_add_fusion), channel_id=1, source_target_pairs={{0,8},{8,0},{16,24},{24,16},{1,9},{9,1},{17,25},{25,17},{2,10},{10... | collective-permute-start | bytes 6152 | tf_op jit(solution)/shard_map/ppermute | solution.py:733
  97.9 20.3 %collective-permute-start.14 = (bf16[128,896]{1,0:T(8,128)(2,1)S(1)}, bf16[128,896]{1,0:T(8,128)(2,1)S(1)}, u32[]{:S(2)}, u32[]{:S(2)}) collective-permute-start(bf16[128,896]{1,0:T(8,128)(2,1)S(1)} %last_norm.1.refs_0_), channel_id=1, source_target_pairs={{0,1},{1,0},{2,3},{3,2},{4,5},{5,4},{6,7},{7,6},{8,9},{9,8},{10,11... | collective-permute-start | bytes 688136 | tf_op jit(solution)/shard_map/ppermute | solution.py:639
  99.0 20.3 %collective-permute-start.15 = (bf16[128,896]{1,0:T(8,128)(2,1)S(1)}, bf16[128,896]{1,0:T(8,128)(2,1)S(1)}, u32[]{:S(2)}, u32[]{:S(2)}) collective-permute-start(bf16[128,896]{1,0:T(8,128)(2,1)S(1)} %last_norm.1.refs_0_), channel_id=1, source_target_pairs={{0,2},{1,3},{2,0},{3,1},{4,6},{5,7},{6,4},{7,5},{8,10},{9,11},{10,... | collective-permute-start | bytes 688136 | tf_op jit(solution)/shard_map/ppermute | solution.py:639
  100.0 7.7 %collective-permute-start.16 = (bf16[128,896]{1,0:T(8,128)(2,1)S(1)}, bf16[128,896]{1,0:T(8,128)(2,1)S(1)}, u32[]{:S(2)}, u32[]{:S(2)}) collective-permute-start(bf16[128,896]{1,0:T(8,128)(2,1)S(1)} %last_norm.1.refs_0_), channel_id=1, source_target_pairs={{0,3},{1,2},{2,1},{3,0},{4,7},{5,6},{6,5},{7,4},{8,11},{9,10},{10,... | collective-permute-start | bytes 688136 | tf_op jit(solution)/shard_map/ppermute | solution.py:639
  103.2 14.1 %collective-permute-start.19 = (bf16[128,896]{1,0:T(8,128)(2,1)S(1)}, bf16[128,896]{1,0:T(8,128)(2,1)S(1)}, u32[]{:S(2)}, u32[]{:S(2)}) collective-permute-start(bf16[128,896]{1,0:T(8,128)(2,1)S(1)} %last_norm.1.refs_0_), channel_id=1, source_target_pairs={{0,16},{8,24},{16,0},{24,8},{1,17},{9,25},{17,1},{25,9},{2,18},{10... | collective-permute-start | bytes 688136 | tf_op jit(solution)/shard_map/ppermute | solution.py:733
  107.7 27.4 %collective-permute-start.24 = (bf16[128,896]{1,0:T(8,128)(2,1)S(1)}, bf16[128,896]{1,0:T(8,128)(2,1)S(1)}, u32[]{:S(2)}, u32[]{:S(2)}) collective-permute-start(bf16[128,896]{1,0:T(8,128)(2,1)S(1)} %last_norm.1.refs_0_), channel_id=1, source_target_pairs={{0,8},{8,0},{16,24},{24,16},{1,9},{9,1},{17,25},{25,17},{2,10},{10... | collective-permute-start | bytes 688136 | tf_op jit(solution)/shard_map/ppermute | solution.py:733
  117.3 19.0 %collective-permute-start.20 = (bf16[128,896]{1,0:T(8,128)(2,1)S(1)}, bf16[128,896]{1,0:T(8,128)(2,1)S(1)}, u32[]{:S(2)}, u32[]{:S(2)}) collective-permute-start(bf16[128,896]{1,0:T(8,128)(2,1)S(1)} %collective-permute-done.19.refs_0_), channel_id=1, source_target_pairs={{0,1},{1,0},{2,3},{3,2},{4,5},{5,4},{6,7},{7,6},{8,9},{9,8},{10,11... | collective-permute-start | bytes 688136 | tf_op jit(solution)/shard_map/ppermute | solution.py:639
  118.3 19.0 %collective-permute-start.21 = (bf16[128,896]{1,0:T(8,128)(2,1)S(1)}, bf16[128,896]{1,0:T(8,128)(2,1)S(1)}, u32[]{:S(2)}, u32[]{:S(2)}) collective-permute-start(bf16[128,896]{1,0:T(8,128)(2,1)S(1)} %collective-permute-done.19.refs_0_), channel_id=1, source_target_pairs={{0,2},{1,3},{2,0},{3,1},{4,6},{5,7},{6,4},{7,5},{8,10},{9,11},{10,... | collective-permute-start | bytes 688136 | tf_op jit(solution)/shard_map/ppermute | solution.py:639
  119.3 19.4 %collective-permute-start.22 = (bf16[128,896]{1,0:T(8,128)(2,1)S(1)}, bf16[128,896]{1,0:T(8,128)(2,1)S(1)}, u32[]{:S(2)}, u32[]{:S(2)}) collective-permute-start(bf16[128,896]{1,0:T(8,128)(2,1)S(1)} %collective-permute-done.19.refs_0_), channel_id=1, source_target_pairs={{0,3},{1,2},{2,1},{3,0},{4,7},{5,6},{6,5},{7,4},{8,11},{9,10},{10,... | collective-permute-start | bytes 688136 | tf_op jit(solution)/shard_map/ppermute | solution.py:639
  120.8 30.4 %collective-permute-start.29 = (bf16[128,896]{1,0:T(8,128)(2,1)S(1)}, bf16[128,896]{1,0:T(8,128)(2,1)S(1)}, u32[]{:S(2)}, u32[]{:S(2)}) collective-permute-start(bf16[128,896]{1,0:T(8,128)(2,1)S(1)} %last_norm.1.refs_0_), channel_id=1, source_target_pairs={{0,24},{8,16},{16,8},{24,0},{1,25},{9,17},{17,9},{25,1},{2,26},{10... | collective-permute-start | bytes 688136 | tf_op jit(solution)/shard_map/ppermute | solution.py:733
  135.1 18.2 %collective-permute-start.25 = (bf16[128,896]{1,0:T(8,128)(2,1)S(1)}, bf16[128,896]{1,0:T(8,128)(2,1)S(1)}, u32[]{:S(2)}, u32[]{:S(2)}) collective-permute-start(bf16[128,896]{1,0:T(8,128)(2,1)S(1)} %collective-permute-done.24.refs_0_), channel_id=1, source_target_pairs={{0,1},{1,0},{2,3},{3,2},{4,5},{5,4},{6,7},{7,6},{8,9},{9,8},{10,11... | collective-permute-start | bytes 688136 | tf_op jit(solution)/shard_map/ppermute | solution.py:639
  136.2 18.6 %collective-permute-start.26 = (bf16[128,896]{1,0:T(8,128)(2,1)S(1)}, bf16[128,896]{1,0:T(8,128)(2,1)S(1)}, u32[]{:S(2)}, u32[]{:S(2)}) collective-permute-start(bf16[128,896]{1,0:T(8,128)(2,1)S(1)} %collective-permute-done.24.refs_0_), channel_id=1, source_target_pairs={{0,2},{1,3},{2,0},{3,1},{4,6},{5,7},{6,4},{7,5},{8,10},{9,11},{10,... | collective-permute-start | bytes 688136 | tf_op jit(solution)/shard_map/ppermute | solution.py:639
  137.3 17.5 %collective-permute-start.27 = (bf16[128,896]{1,0:T(8,128)(2,1)S(1)}, bf16[128,896]{1,0:T(8,128)(2,1)S(1)}, u32[]{:S(2)}, u32[]{:S(2)}) collective-permute-start(bf16[128,896]{1,0:T(8,128)(2,1)S(1)} %collective-permute-done.24.refs_0_), channel_id=1, source_target_pairs={{0,3},{1,2},{2,1},{3,0},{4,7},{5,6},{6,5},{7,4},{8,11},{9,10},{10,... | collective-permute-start | bytes 688136 | tf_op jit(solution)/shard_map/ppermute | solution.py:639
  151.2 16.1 %collective-permute-start.30 = (bf16[128,896]{1,0:T(8,128)(2,1)S(1)}, bf16[128,896]{1,0:T(8,128)(2,1)S(1)}, u32[]{:S(2)}, u32[]{:S(2)}) collective-permute-start(bf16[128,896]{1,0:T(8,128)(2,1)S(1)} %collective-permute-done.29.refs_0_), channel_id=1, source_target_pairs={{0,1},{1,0},{2,3},{3,2},{4,5},{5,4},{6,7},{7,6},{8,9},{9,8},{10,11... | collective-permute-start | bytes 688136 | tf_op jit(solution)/shard_map/ppermute | solution.py:639
  152.3 15.0 %collective-permute-start.31 = (bf16[128,896]{1,0:T(8,128)(2,1)S(1)}, bf16[128,896]{1,0:T(8,128)(2,1)S(1)}, u32[]{:S(2)}, u32[]{:S(2)}) collective-permute-start(bf16[128,896]{1,0:T(8,128)(2,1)S(1)} %collective-permute-done.29.refs_0_), channel_id=1, source_target_pairs={{0,2},{1,3},{2,0},{3,1},{4,6},{5,7},{6,4},{7,5},{8,10},{9,11},{10,... | collective-permute-start | bytes 688136 | tf_op jit(solution)/shard_map/ppermute | solution.py:639
  153.3 14.0 %collective-permute-start.32 = (bf16[128,896]{1,0:T(8,128)(2,1)S(1)}, bf16[128,896]{1,0:T(8,128)(2,1)S(1)}, u32[]{:S(2)}, u32[]{:S(2)}) collective-permute-start(bf16[128,896]{1,0:T(8,128)(2,1)S(1)} %collective-permute-done.29.refs_0_), channel_id=1, source_target_pairs={{0,3},{1,2},{2,1},{3,0},{4,7},{5,6},{6,5},{7,4},{8,11},{9,10},{10,... | collective-permute-start | bytes 688136 | tf_op jit(solution)/shard_map/ppermute | solution.py:639
  181.1 11.6 %all-to-all-start = ((f32[16,3,128]{2,1,0:T(4,128)}), f32[16,3,128]{2,1,0:T(4,128)S(1)}, u32[]{:S(2)}, u32[]{:S(2)}) async-start(f32[16,3,128]{2,1,0:T(4,128)} %gather_fusion), calls=%async_computation | async-start | bytes 65536 | tf_op jit(solution)/shard_map/all_to_all | solution.py:771
  (8 other events, 119.3 us)

commit v3 on v2

--- a/solution.py
+++ b/solution.py
@@ -720,7 +720,7 @@
     final = last_norm(h, parts, tall(final_gain))
 
     zq_count = lax.axis_size("zq")
-    turns = [(q, p) for q in range(zq_count) for p in range(zp_count)]
+    turns = [(q, p) for p in range(zp_count) for q in range(zq_count)]
 
     def brought(x, turn):
         if turn == (0, 0):
@@ -764,8 +764,8 @@
     place_zp = jnp.arange(zp_count)[:, None, None]
     place_zq = jnp.arange(zq_count)[None, :, None]
     place_t = jnp.arange(tp_count)[None, None, :]
-    at = (lax.axis_index("zq") - place_zq) % zq_count * zp_count
-    at = (at + (lax.axis_index("zp") - place_zp) % zp_count) * tp_count
+    at = (lax.axis_index("zp") - place_zp) % zp_count * zq_count
+    at = (at + (lax.axis_index("zq") - place_zq) % zq_count) * tp_count
     at = at + (place_t ^ column if direct else place_t)
     stats = jnp.take(stats, at.reshape(-1), axis=0, mode="clip")
     stats = lax.all_to_all(stats, ("zp", "zq", "tensor"), 0, 0, tiled=False)

time: 203 us -> 200 us (0.985)
  waiting for transfers between devices: 29.1 us -> 25.7 us
    ppermute x6, waiting for transfers between devices: 6.99 us -> 2.79 us  [brought(): return lax.ppermute(x, ('zp', 'zq'), route)]
where the time goes in v3:
time: 200 us; the launch traced here: 199 us
  Pallas kernels  84.4 us (42%)
  starting transfers between devices  49.5 us (25%)
  blocking collectives  29.2 us (15%)
  waiting for transfers between devices  25.7 us (13%)
  local copies, waits for them, and re-layouts  5.59 us (3%)
  other arithmetic  3.26 us (2%)
    pallas_call x4, Pallas kernels, head_stats_mxu(): pl.pallas_call(body, grid=(1,), out_shape=jax.ShapeDtypeStruct((8, count)...  50 us
    ppermute x24, starting transfers between devices, peer(): return lax.ppermute(x, 'tensor', [(i, i ^ k) for i in range(tp_count)])  28.7 us
    all_gather x2, blocking collectives, on_device(): kv = lax.all_gather(kv, 'tensor', axis=1, tiled=True)  20.3 us
    ppermute x24, waiting for transfers between devices, peer(): return lax.ppermute(x, 'tensor', [(i, i ^ k) for i in range(tp_count)])  15.5 us
    ppermute x6, starting transfers between devices, brought(): return lax.ppermute(x, ('zp', 'zq'), route)  10.9 us
    pallas_call x6, Pallas kernels, mlp_kept(): pl.pallas_call(body, grid=(1,), out_shape=jax.ShapeDtypeStruct(x.shape, B...  10.9 us
    pallas_call x2, Pallas kernels, mlp_load(): pl.pallas_call(body, grid=(1,), out_shape=[jax.ShapeDtypeStruct(x.shape,...  9.55 us
    all_to_all x1, blocking collectives, on_device(): lax.all_to_all(spread, ALL, 0, 0, tiled=False)  8.9 us
  transfers between devices with their start and end apart: 34, of which 8 were waited for; matrix products, arithmetic and copies ran while one was open for 1% of the time, Pallas kernels for 35%

profile of v3, /device:TPU:0, one launch (start us, length us, event | category | flops | bytes accessed | tf_op | source)
XLA Modules:
  0.0 198.8 jit_solution(2773576440664421957)
XLA Ops:
  6.2 2.4 %collective-permute-start = (bf16[3,32,256]{2,1,0:T(8,128)(2,1)S(1)}, bf16[3,32,256]{2,1,0:T(8,128)(2,1)S(1)}, u32[]{:S(2)}, u32[]{:S(2)}) collective-permute-start(bf16[3,32,256]{2,1,0:T(8,128)(2,1)S(1)} %bitcast.73), channel_id=1, source_target_pairs={{0,4},{4,8},{8,12},{12,16},{16,20},{20,24},{24,28},{1,5},{5,9},{9,... | collective-permute-start | bytes 147464 | tf_op jit(solution)/shard_map/ppermute | solution.py:601
  8.6 2.7 %collective-permute-start.17 = (bf16[896,3072]{1,0:T(8,128)(2,1)}, bf16[896,3072]{1,0:T(8,128)(2,1)}, u32[]{:S(2)}, u32[]{:S(2)}) collective-permute-start(bf16[896,3072]{1,0:T(8,128)(2,1)} %refs_4_.7), channel_id=1, source_target_pairs={{0,4},{4,0},{1,5},{5,1},{2,6},{6,2},{3,7},{7,3},{8,12},{12,8},{9,1... | collective-permute-start | bytes 16515080 | tf_op jit(solution)/shard_map/ppermute | solution.py:643
  12.9 2.0 %queries.2.refs_2_ = bf16[128,896]{1,0:T(8,128)(2,1)S(1)} custom-call(bf16[128,896]{1,0:T(8,128)(2,1)S(1)} %get-tuple-element.32.a_ref, bf16[2,896,896]{2,1,0:T(8,128)(2,1)} %w_ref.3, f32[128,128]{1,0:T(8,128)S(1)} %get-tuple-element.71.refs_4_.cos_ref.refs_8_, f32[128,128]{1,0:T(8,128)S(1)} %get-tuple-element.70.refs_5_.sin_ref.refs_9_), custom_call_target="tpu_custom_call" | custom-call | flops 205520896 | tf_op jit(solution)/shard_map/queries/pallas_call | solution.py:147
  15.0 10.0 %all_gather.6 = bf16[8,128,256]{2,1,0:T(8,128)(2,1)S(1)} all-gather(bf16[8,32,256]{2,1,0:T(8,128)(2,1)S(1)} %pad_maximum_fusion), channel_id=1, replica_groups=mesh['zp'=2,'zq'=2,'core'=2,'tensor'=4] {'tensor'}, dimensions={1}, use_global_device_ids=true | all-gather | bytes 655360 | tf_op jit(solution)/shard_map/all_gather | solution.py:691
  25.1 3.1 %attention.2 = (f32[128,896]{1,0:T(8,128)S(1)}, bf16[128,896]{1,0:T(8,128)(2,1)S(1)}) custom-call(bf16[384,256]{1,0:T(8,128)(2,1)S(1)} %bitcast.58, bf16[512,256]{1,0:T(8,128)(2,1)S(1)} %bitcast.56, bf16[128,896]{1,0:T(8,128)(2,1)S(1)} %queries.2.refs_2_, f32[4,32,512]{2,1,0:T(8,128)S(1)} %and_select_fusion.refs_3_, ...), custom_call_target="tpu_custom_call" | custom-call | flops 675282944 | tf_op jit(solution)/shard_map/attention/pallas_call | solution.py:249
  28.2 1.6 collective-permute-start.1
  31.8 4.8 %mlp_load.2 = (f32[128,896]{1,0:T(8,128)S(1)}, bf16[1216,896]{1,0:T(8,128)(2,1)S(1)}, bf16[1216,896]{1,0:T(8,128)(2,1)S(1)}, bf16[1216,896]{1,0:T(8,128)(2,1)S(1)}) custom-call(bf16[128,896]{1,0:T(8,128)(2,1)S(1)} %get-tuple-element.35.x_ref, bf16[2,1216,896]{2,1,0:T(8,128)(2,1)} %bitcast.66, bf16[2,1216,896]{2,1,0:T(8,128)(2,1)} %bitcast.68, ...), custom_call_target="tpu_custom_call" | custom-call | flops 836763648 | tf_op jit(solution)/shard_map/mlp_load/pallas_call | solution.py:318
  36.6 1.8 mlp_kept.6
  38.4 1.6 collective-permute-start.2
  40.0 1.8 mlp_kept.7
  42.4 1.8 mlp_kept.8
  45.9 6.4 %collective-permute-done.4.refs_3_ = bf16[128,896]{1,0:T(8,128)(2,1)S(1)} collective-permute-done((bf16[128,896]{1,0:T(8,128)(2,1)S(1)}, bf16[128,896]{1,0:T(8,128)(2,1)S(1)}, u32[]{:S(2)}, u32[]{:S(2)}) %collective-permute-start.4) | collective-permute-done | bytes 229408 | tf_op jit(solution)/shard_map/ppermute | solution.py:639
  55.1 2.0 %queries.3.refs_2_ = bf16[128,896]{1,0:T(8,128)(2,1)S(1)} custom-call(bf16[128,896]{1,0:T(8,128)(2,1)S(1)} %get-tuple-element.41.a_ref, bf16[2,896,896]{2,1,0:T(8,128)(2,1)} %w_ref.3, f32[128,128]{1,0:T(8,128)S(1)} %get-tuple-element.71.refs_4_.cos_ref.refs_8_, f32[128,128]{1,0:T(8,128)S(1)} %get-tuple-element.70.refs_5_.sin_ref.refs_9_), custom_call_target="tpu_custom_call" | custom-call | flops 205520896 | tf_op jit(solution)/shard_map/queries/pallas_call | solution.py:147
  57.2 10.2 %all_gather.7 = bf16[7,128,256]{2,1,0:T(8,128)(2,1)S(1)} all-gather(bf16[7,32,256]{2,1,0:T(8,128)(2,1)S(1)} %pad_maximum_fusion.1), channel_id=1, replica_groups=mesh['zp'=2,'zq'=2,'core'=2,'tensor'=4] {'tensor'}, dimensions={1}, use_global_device_ids=true | all-gather | bytes 573440 | tf_op jit(solution)/shard_map/all_gather | solution.py:691
  67.4 3.7 %attention.3 = (f32[128,896]{1,0:T(8,128)S(1)}, bf16[128,896]{1,0:T(8,128)(2,1)S(1)}) custom-call(bf16[384,256]{1,0:T(8,128)(2,1)S(1)} %bitcast.57, bf16[512,256]{1,0:T(8,128)(2,1)S(1)} %bitcast.55, bf16[128,896]{1,0:T(8,128)(2,1)S(1)} %queries.3.refs_2_, f32[4,32,512]{2,1,0:T(8,128)S(1)} %and_select_fusion.refs_3_, ...), custom_call_target="tpu_custom_call" | custom-call | flops 675282944 | tf_op jit(solution)/shard_map/attention/pallas_call | solution.py:249
  74.7 4.8 %mlp_load.3 = (f32[128,896]{1,0:T(8,128)S(1)}, bf16[1216,896]{1,0:T(8,128)(2,1)S(1)}, bf16[1216,896]{1,0:T(8,128)(2,1)S(1)}, bf16[1216,896]{1,0:T(8,128)(2,1)S(1)}) custom-call(bf16[128,896]{1,0:T(8,128)(2,1)S(1)} %get-tuple-element.44.x_ref, bf16[2,1216,896]{2,1,0:T(8,128)(2,1)} %bitcast.67, bf16[2,1216,896]{2,1,0:T(8,128)(2,1)} %bitcast.69, ...), custom_call_target="tpu_custom_call" | custom-call | flops 836763648 | tf_op jit(solution)/shard_map/mlp_load/pallas_call | solution.py:318
  79.7 1.8 mlp_kept.9
  82.6 1.8 collective-permute-done.10.x_ref
  84.4 1.8 mlp_kept.10
  87.3 1.8 mlp_kept.11
  91.7 2.6 %collective-permute-start.23 = (s32[4,128]{1,0:T(4,128)S(1)}, s32[4,128]{1,0:T(4,128)S(1)}, u32[]{:S(2)}, u32[]{:S(2)}) collective-permute-start(s32[4,128]{1,0:T(4,128)S(1)} %pad_add_fusion), channel_id=1, source_target_pairs={{0,16},{8,24},{16,0},{24,8},{1,17},{9,25},{17,1},{25,9},{2,18},{10... | collective-permute-start | bytes 6152 | tf_op jit(solution)/shard_map/ppermute | solution.py:733
  94.2 3.4 %collective-permute-done.11.refs_2_ = bf16[128,896]{1,0:T(8,128)(2,1)S(1)} collective-permute-done((bf16[128,896]{1,0:T(8,128)(2,1)S(1)}, bf16[128,896]{1,0:T(8,128)(2,1)S(1)}, u32[]{:S(2)}, u32[]{:S(2)}) %collective-permute-start.11) | collective-permute-done | bytes 229408 | tf_op jit(solution)/shard_map/ppermute | solution.py:639
  104.7 3.7 %collective-permute-done.16.refs_3_ = bf16[128,896]{1,0:T(8,128)(2,1)S(1)} collective-permute-done((bf16[128,896]{1,0:T(8,128)(2,1)S(1)}, bf16[128,896]{1,0:T(8,128)(2,1)S(1)}, u32[]{:S(2)}, u32[]{:S(2)}) %collective-permute-start.16) | collective-permute-done | bytes 229408 | tf_op jit(solution)/shard_map/ppermute | solution.py:639
  108.3 4.0 %collective-permute-start.24 = (bf16[128,896]{1,0:T(8,128)(2,1)S(1)}, bf16[128,896]{1,0:T(8,128)(2,1)S(1)}, u32[]{:S(2)}, u32[]{:S(2)}) collective-permute-start(bf16[128,896]{1,0:T(8,128)(2,1)S(1)} %last_norm.1.refs_0_), channel_id=1, source_target_pairs={{0,16},{8,24},{16,0},{24,8},{1,17},{9,25},{17,1},{25,9},{2,18},{10... | collective-permute-start | bytes 688136 | tf_op jit(solution)/shard_map/ppermute | solution.py:733
  117.0 2.6 %collective-permute-start.29 = (bf16[128,896]{1,0:T(8,128)(2,1)S(1)}, bf16[128,896]{1,0:T(8,128)(2,1)S(1)}, u32[]{:S(2)}, u32[]{:S(2)}) collective-permute-start(bf16[128,896]{1,0:T(8,128)(2,1)S(1)} %last_norm.1.refs_0_), channel_id=1, source_target_pairs={{0,24},{8,16},{16,8},{24,0},{1,25},{9,17},{17,9},{25,1},{2,26},{10... | collective-permute-start | bytes 688136 | tf_op jit(solution)/shard_map/ppermute | solution.py:733
  119.7 12.5 %head_stats_mxu.4 = f32[8,512]{1,0:T(8,128)S(1)} custom-call(s32[2]{0:T(128)S(1)} %pad_add_fusion.2.base_ref, s32[512,1]{1,0:T(8,128)S(1)} %copy.32.want_ref, bf16[128,896]{1,0:T(8,128)(2,1)S(1)} %last_norm.1.refs_0_, bf16[128,896]{1,0:T(8,128)(2,1)S(1)} %collective-permute-done.14.refs_1_, bf16[128,896]{1,0:T(8,128)(2,1)S(1)} %collective-permute-done.15.refs_2_, ...), custom_call_target="tpu_custom_call" | custom-call | flops 5637144576 | tf_op jit(solution)/shard_map/head_stats_mxu/pallas_call | solution.py:575
  135.7 12.5 %head_stats_mxu.5 = f32[8,512]{1,0:T(8,128)S(1)} custom-call(s32[2]{0:T(128)S(1)} %pad_add_fusion.2.base_ref, s32[512,1]{1,0:T(8,128)S(1)} %copy.33.want_ref, bf16[128,896]{1,0:T(8,128)(2,1)S(1)} %collective-permute-done.19.refs_0_, bf16[128,896]{1,0:T(8,128)(2,1)S(1)} %collective-permute-done.20.refs_1_, ...), custom_call_target="tpu_custom_call" | custom-call | flops 5637144576 | tf_op jit(solution)/shard_map/head_stats_mxu/pallas_call | solution.py:575
  151.8 12.5 %head_stats_mxu.6 = f32[8,512]{1,0:T(8,128)S(1)} custom-call(s32[2]{0:T(128)S(1)} %pad_add_fusion.2.base_ref, s32[512,1]{1,0:T(8,128)S(1)} %copy.34.want_ref, bf16[128,896]{1,0:T(8,128)(2,1)S(1)} %collective-permute-done.24.refs_0_, bf16[128,896]{1,0:T(8,128)(2,1)S(1)} %collective-permute-done.25.refs_1_, ...), custom_call_target="tpu_custom_call" | custom-call | flops 5637144576 | tf_op jit(solution)/shard_map/head_stats_mxu/pallas_call | solution.py:575
  164.4 12.5 %head_stats_mxu.7 = f32[8,512]{1,0:T(8,128)S(1)} custom-call(s32[2]{0:T(128)S(1)} %pad_add_fusion.2.base_ref, s32[512,1]{1,0:T(8,128)S(1)} %copy.35.want_ref, bf16[128,896]{1,0:T(8,128)(2,1)S(1)} %collective-permute-done.29.refs_0_, bf16[128,896]{1,0:T(8,128)(2,1)S(1)} %collective-permute-done.30.refs_1_, ...), custom_call_target="tpu_custom_call" | custom-call | flops 5637144576 | tf_op jit(solution)/shard_map/head_stats_mxu/pallas_call | solution.py:575
  178.1 3.5 %all-to-all-start = ((f32[16,3,128]{2,1,0:T(4,128)}), f32[16,3,128]{2,1,0:T(4,128)S(1)}, u32[]{:S(2)}, u32[]{:S(2)}) async-start(f32[16,3,128]{2,1,0:T(4,128)} %gather_fusion), calls=%async_computation | async-start | bytes 65536 | tf_op jit(solution)/shard_map/all_to_all | solution.py:771
  181.6 7.4 %all-to-all-done = f32[16,3,128]{2,1,0:T(4,128)S(1)} async-done(((f32[16,3,128]{2,1,0:T(4,128)}), f32[16,3,128]{2,1,0:T(4,128)S(1)}, u32[]{:S(2)}, u32[]{:S(2)}) %all-to-all-start) | async-done | bytes 24608 | tf_op jit(solution)/shard_map/all_to_all | solution.py:771
  189.4 8.9 %all_to_all.11 = f32[32,1,128]{2,1,0:T(1,128)S(1)} all-to-all(f32[32,1,128]{2,1,0:T(1,128)S(1)} %broadcast_in_dim.152), channel_id=1, replica_groups=mesh['zp'=2,'zq'=2,'core'=2,'tensor'=4] {'zp','zq','core','tensor'}, dimensions={0} | all-to-all | bytes 32768 | tf_op jit(solution)/shard_map/all_to_all | solution.py:782
  (144 shorter events, 43.6 us)
Async XLA Ops:
  6.2 8.7 %collective-permute-start = (bf16[3,32,256]{2,1,0:T(8,128)(2,1)S(1)}, bf16[3,32,256]{2,1,0:T(8,128)(2,1)S(1)}, u32[]{:S(2)}, u32[]{:S(2)}) collective-permute-start(bf16[3,32,256]{2,1,0:T(8,128)(2,1)S(1)} %bitcast.73), channel_id=1, source_target_pairs={{0,4},{4,8},{8,12},{12,16},{16,20},{20,24},{24,28},{1,5},{5,9},{9,... | collective-permute-start | bytes 147464 | tf_op jit(solution)/shard_map/ppermute | solution.py:601
  8.6 108.4 %collective-permute-start.17 = (bf16[896,3072]{1,0:T(8,128)(2,1)}, bf16[896,3072]{1,0:T(8,128)(2,1)}, u32[]{:S(2)}, u32[]{:S(2)}) collective-permute-start(bf16[896,3072]{1,0:T(8,128)(2,1)} %refs_4_.7), channel_id=1, source_target_pairs={{0,4},{4,0},{1,5},{5,1},{2,6},{6,2},{3,7},{7,3},{8,12},{12,8},{9,1... | collective-permute-start | bytes 16515080 | tf_op jit(solution)/shard_map/ppermute | solution.py:643
  28.2 8.3 %collective-permute-start.1 = (bf16[128,896]{1,0:T(8,128)(2,1)S(1)}, bf16[128,896]{1,0:T(8,128)(2,1)S(1)}, u32[]{:S(2)}, u32[]{:S(2)}) collective-permute-start(bf16[128,896]{1,0:T(8,128)(2,1)S(1)} %get-tuple-element.35.x_ref), channel_id=1, source_target_pairs={{0,1},{1,0},{2,3},{3,2},{4,5},{5,4},{6,7},{7,6},{8,9},{9,8},{10,11... | collective-permute-start | bytes 688136 | tf_op jit(solution)/shard_map/ppermute | solution.py:639
  29.8 10.2 %collective-permute-start.3 = (bf16[128,896]{1,0:T(8,128)(2,1)S(1)}, bf16[128,896]{1,0:T(8,128)(2,1)S(1)}, u32[]{:S(2)}, u32[]{:S(2)}) collective-permute-start(bf16[128,896]{1,0:T(8,128)(2,1)S(1)} %get-tuple-element.35.x_ref), channel_id=1, source_target_pairs={{0,2},{1,3},{2,0},{3,1},{4,6},{5,7},{6,4},{7,5},{8,10},{9,11},{10,... | collective-permute-start | bytes 688136 | tf_op jit(solution)/shard_map/ppermute | solution.py:639
  30.3 12.0 %collective-permute-start.5 = (bf16[128,896]{1,0:T(8,128)(2,1)S(1)}, bf16[128,896]{1,0:T(8,128)(2,1)S(1)}, u32[]{:S(2)}, u32[]{:S(2)}) collective-permute-start(bf16[128,896]{1,0:T(8,128)(2,1)S(1)} %get-tuple-element.35.x_ref), channel_id=1, source_target_pairs={{0,3},{1,2},{2,1},{3,0},{4,7},{5,6},{6,5},{7,4},{8,11},{9,10},{10,... | collective-permute-start | bytes 688136 | tf_op jit(solution)/shard_map/ppermute | solution.py:639
  38.4 7.5 %collective-permute-start.2 = (bf16[128,896]{1,0:T(8,128)(2,1)S(1)}, bf16[128,896]{1,0:T(8,128)(2,1)S(1)}, u32[]{:S(2)}, u32[]{:S(2)}) collective-permute-start(bf16[128,896]{1,0:T(8,128)(2,1)S(1)} %mlp_kept.6), channel_id=1, source_target_pairs={{0,1},{1,0},{2,3},{3,2},{4,5},{5,4},{6,7},{7,6},{8,9},{9,8},{10,11... | collective-permute-start | bytes 688136 | tf_op jit(solution)/shard_map/ppermute | solution.py:639
  41.8 10.5 %collective-permute-start.4 = (bf16[128,896]{1,0:T(8,128)(2,1)S(1)}, bf16[128,896]{1,0:T(8,128)(2,1)S(1)}, u32[]{:S(2)}, u32[]{:S(2)}) collective-permute-start(bf16[128,896]{1,0:T(8,128)(2,1)S(1)} %mlp_kept.7), channel_id=1, source_target_pairs={{0,2},{1,3},{2,0},{3,1},{4,6},{5,7},{6,4},{7,5},{8,10},{9,11},{10,... | collective-permute-start | bytes 688136 | tf_op jit(solution)/shard_map/ppermute | solution.py:639
  44.2 8.0 %collective-permute-start.6 = (bf16[128,896]{1,0:T(8,128)(2,1)S(1)}, bf16[128,896]{1,0:T(8,128)(2,1)S(1)}, u32[]{:S(2)}, u32[]{:S(2)}) collective-permute-start(bf16[128,896]{1,0:T(8,128)(2,1)S(1)} %mlp_kept.8), channel_id=1, source_target_pairs={{0,3},{1,2},{2,1},{3,0},{4,7},{5,6},{6,5},{7,4},{8,11},{9,10},{10,... | collective-permute-start | bytes 688136 | tf_op jit(solution)/shard_map/ppermute | solution.py:639
  71.1 8.5 %collective-permute-start.8 = (bf16[128,896]{1,0:T(8,128)(2,1)S(1)}, bf16[128,896]{1,0:T(8,128)(2,1)S(1)}, u32[]{:S(2)}, u32[]{:S(2)}) collective-permute-start(bf16[128,896]{1,0:T(8,128)(2,1)S(1)} %get-tuple-element.44.x_ref), channel_id=1, source_target_pairs={{0,1},{1,0},{2,3},{3,2},{4,5},{5,4},{6,7},{7,6},{8,9},{9,8},{10,11... | collective-permute-start | bytes 688136 | tf_op jit(solution)/shard_map/ppermute | solution.py:639
  72.2 12.2 %collective-permute-start.10 = (bf16[128,896]{1,0:T(8,128)(2,1)S(1)}, bf16[128,896]{1,0:T(8,128)(2,1)S(1)}, u32[]{:S(2)}, u32[]{:S(2)}) collective-permute-start(bf16[128,896]{1,0:T(8,128)(2,1)S(1)} %get-tuple-element.44.x_ref), channel_id=1, source_target_pairs={{0,2},{1,3},{2,0},{3,1},{4,6},{5,7},{6,4},{7,5},{8,10},{9,11},{10,... | collective-permute-start | bytes 688136 | tf_op jit(solution)/shard_map/ppermute | solution.py:639
  73.2 14.1 %collective-permute-start.12 = (bf16[128,896]{1,0:T(8,128)(2,1)S(1)}, bf16[128,896]{1,0:T(8,128)(2,1)S(1)}, u32[]{:S(2)}, u32[]{:S(2)}) collective-permute-start(bf16[128,896]{1,0:T(8,128)(2,1)S(1)} %get-tuple-element.44.x_ref), channel_id=1, source_target_pairs={{0,3},{1,2},{2,1},{3,0},{4,7},{5,6},{6,5},{7,4},{8,11},{9,10},{10,... | collective-permute-start | bytes 688136 | tf_op jit(solution)/shard_map/ppermute | solution.py:639
  81.5 10.2 %collective-permute-start.9 = (bf16[128,896]{1,0:T(8,128)(2,1)S(1)}, bf16[128,896]{1,0:T(8,128)(2,1)S(1)}, u32[]{:S(2)}, u32[]{:S(2)}) collective-permute-start(bf16[128,896]{1,0:T(8,128)(2,1)S(1)} %mlp_kept.9), channel_id=1, source_target_pairs={{0,1},{1,0},{2,3},{3,2},{4,5},{5,4},{6,7},{7,6},{8,9},{9,8},{10,11... | collective-permute-start | bytes 688136 | tf_op jit(solution)/shard_map/ppermute | solution.py:639
  86.2 11.4 %collective-permute-start.11 = (bf16[128,896]{1,0:T(8,128)(2,1)S(1)}, bf16[128,896]{1,0:T(8,128)(2,1)S(1)}, u32[]{:S(2)}, u32[]{:S(2)}) collective-permute-start(bf16[128,896]{1,0:T(8,128)(2,1)S(1)} %mlp_kept.10), channel_id=1, source_target_pairs={{0,2},{1,3},{2,0},{3,1},{4,6},{5,7},{6,4},{7,5},{8,10},{9,11},{10,... | collective-permute-start | bytes 688136 | tf_op jit(solution)/shard_map/ppermute | solution.py:639
  89.1 8.6 %collective-permute-start.13 = (bf16[128,896]{1,0:T(8,128)(2,1)S(1)}, bf16[128,896]{1,0:T(8,128)(2,1)S(1)}, u32[]{:S(2)}, u32[]{:S(2)}) collective-permute-start(bf16[128,896]{1,0:T(8,128)(2,1)S(1)} %mlp_kept.11), channel_id=1, source_target_pairs={{0,3},{1,2},{2,1},{3,0},{4,7},{5,6},{6,5},{7,4},{8,11},{9,10},{10,... | collective-permute-start | bytes 688136 | tf_op jit(solution)/shard_map/ppermute | solution.py:639
  90.7 8.3 %collective-permute-start.18 = (s32[4,128]{1,0:T(4,128)S(1)}, s32[4,128]{1,0:T(4,128)S(1)}, u32[]{:S(2)}, u32[]{:S(2)}) collective-permute-start(s32[4,128]{1,0:T(4,128)S(1)} %pad_add_fusion), channel_id=1, source_target_pairs={{0,8},{8,0},{16,24},{24,16},{1,9},{9,1},{17,25},{25,17},{2,10},{10... | collective-permute-start | bytes 6152 | tf_op jit(solution)/shard_map/ppermute | solution.py:733
  91.7 8.4 %collective-permute-start.23 = (s32[4,128]{1,0:T(4,128)S(1)}, s32[4,128]{1,0:T(4,128)S(1)}, u32[]{:S(2)}, u32[]{:S(2)}) collective-permute-start(s32[4,128]{1,0:T(4,128)S(1)} %pad_add_fusion), channel_id=1, source_target_pairs={{0,16},{8,24},{16,0},{24,8},{1,17},{9,25},{17,1},{25,9},{2,18},{10... | collective-permute-start | bytes 6152 | tf_op jit(solution)/shard_map/ppermute | solution.py:733
  97.9 16.6 %collective-permute-start.14 = (bf16[128,896]{1,0:T(8,128)(2,1)S(1)}, bf16[128,896]{1,0:T(8,128)(2,1)S(1)}, u32[]{:S(2)}, u32[]{:S(2)}) collective-permute-start(bf16[128,896]{1,0:T(8,128)(2,1)S(1)} %last_norm.1.refs_0_), channel_id=1, source_target_pairs={{0,1},{1,0},{2,3},{3,2},{4,5},{5,4},{6,7},{7,6},{8,9},{9,8},{10,11... | collective-permute-start | bytes 688136 | tf_op jit(solution)/shard_map/ppermute | solution.py:639
  99.0 16.5 %collective-permute-start.15 = (bf16[128,896]{1,0:T(8,128)(2,1)S(1)}, bf16[128,896]{1,0:T(8,128)(2,1)S(1)}, u32[]{:S(2)}, u32[]{:S(2)}) collective-permute-start(bf16[128,896]{1,0:T(8,128)(2,1)S(1)} %last_norm.1.refs_0_), channel_id=1, source_target_pairs={{0,2},{1,3},{2,0},{3,1},{4,6},{5,7},{6,4},{7,5},{8,10},{9,11},{10,... | collective-permute-start | bytes 688136 | tf_op jit(solution)/shard_map/ppermute | solution.py:639
  100.0 8.3 %collective-permute-start.16 = (bf16[128,896]{1,0:T(8,128)(2,1)S(1)}, bf16[128,896]{1,0:T(8,128)(2,1)S(1)}, u32[]{:S(2)}, u32[]{:S(2)}) collective-permute-start(bf16[128,896]{1,0:T(8,128)(2,1)S(1)} %last_norm.1.refs_0_), channel_id=1, source_target_pairs={{0,3},{1,2},{2,1},{3,0},{4,7},{5,6},{6,5},{7,4},{8,11},{9,10},{10,... | collective-permute-start | bytes 688136 | tf_op jit(solution)/shard_map/ppermute | solution.py:639
  103.1 10.5 %collective-permute-start.19 = (bf16[128,896]{1,0:T(8,128)(2,1)S(1)}, bf16[128,896]{1,0:T(8,128)(2,1)S(1)}, u32[]{:S(2)}, u32[]{:S(2)}) collective-permute-start(bf16[128,896]{1,0:T(8,128)(2,1)S(1)} %last_norm.1.refs_0_), channel_id=1, source_target_pairs={{0,8},{8,0},{16,24},{24,16},{1,9},{9,1},{17,25},{25,17},{2,10},{10... | collective-permute-start | bytes 688136 | tf_op jit(solution)/shard_map/ppermute | solution.py:733
  108.3 23.8 %collective-permute-start.24 = (bf16[128,896]{1,0:T(8,128)(2,1)S(1)}, bf16[128,896]{1,0:T(8,128)(2,1)S(1)}, u32[]{:S(2)}, u32[]{:S(2)}) collective-permute-start(bf16[128,896]{1,0:T(8,128)(2,1)S(1)} %last_norm.1.refs_0_), channel_id=1, source_target_pairs={{0,16},{8,24},{16,0},{24,8},{1,17},{9,25},{17,1},{25,9},{2,18},{10... | collective-permute-start | bytes 688136 | tf_op jit(solution)/shard_map/ppermute | solution.py:733
  113.5 19.7 %collective-permute-start.20 = (bf16[128,896]{1,0:T(8,128)(2,1)S(1)}, bf16[128,896]{1,0:T(8,128)(2,1)S(1)}, u32[]{:S(2)}, u32[]{:S(2)}) collective-permute-start(bf16[128,896]{1,0:T(8,128)(2,1)S(1)} %collective-permute-done.19.refs_0_), channel_id=1, source_target_pairs={{0,1},{1,0},{2,3},{3,2},{4,5},{5,4},{6,7},{7,6},{8,9},{9,8},{10,11... | collective-permute-start | bytes 688136 | tf_op jit(solution)/shard_map/ppermute | solution.py:639
  114.5 19.7 %collective-permute-start.21 = (bf16[128,896]{1,0:T(8,128)(2,1)S(1)}, bf16[128,896]{1,0:T(8,128)(2,1)S(1)}, u32[]{:S(2)}, u32[]{:S(2)}) collective-permute-start(bf16[128,896]{1,0:T(8,128)(2,1)S(1)} %collective-permute-done.19.refs_0_), channel_id=1, source_target_pairs={{0,2},{1,3},{2,0},{3,1},{4,6},{5,7},{6,4},{7,5},{8,10},{9,11},{10,... | collective-permute-start | bytes 688136 | tf_op jit(solution)/shard_map/ppermute | solution.py:639
  115.5 20.2 %collective-permute-start.22 = (bf16[128,896]{1,0:T(8,128)(2,1)S(1)}, bf16[128,896]{1,0:T(8,128)(2,1)S(1)}, u32[]{:S(2)}, u32[]{:S(2)}) collective-permute-start(bf16[128,896]{1,0:T(8,128)(2,1)S(1)} %collective-permute-done.19.refs_0_), channel_id=1, source_target_pairs={{0,3},{1,2},{2,1},{3,0},{4,7},{5,6},{6,5},{7,4},{8,11},{9,10},{10,... | collective-permute-start | bytes 688136 | tf_op jit(solution)/shard_map/ppermute | solution.py:639
  117.0 31.2 %collective-permute-start.29 = (bf16[128,896]{1,0:T(8,128)(2,1)S(1)}, bf16[128,896]{1,0:T(8,128)(2,1)S(1)}, u32[]{:S(2)}, u32[]{:S(2)}) collective-permute-start(bf16[128,896]{1,0:T(8,128)(2,1)S(1)} %last_norm.1.refs_0_), channel_id=1, source_target_pairs={{0,24},{8,16},{16,8},{24,0},{1,25},{9,17},{17,9},{25,1},{2,26},{10... | collective-permute-start | bytes 688136 | tf_op jit(solution)/shard_map/ppermute | solution.py:733
  132.2 18.2 %collective-permute-start.25 = (bf16[128,896]{1,0:T(8,128)(2,1)S(1)}, bf16[128,896]{1,0:T(8,128)(2,1)S(1)}, u32[]{:S(2)}, u32[]{:S(2)}) collective-permute-start(bf16[128,896]{1,0:T(8,128)(2,1)S(1)} %collective-permute-done.24.refs_0_), channel_id=1, source_target_pairs={{0,1},{1,0},{2,3},{3,2},{4,5},{5,4},{6,7},{7,6},{8,9},{9,8},{10,11... | collective-permute-start | bytes 688136 | tf_op jit(solution)/shard_map/ppermute | solution.py:639
  133.2 18.6 %collective-permute-start.26 = (bf16[128,896]{1,0:T(8,128)(2,1)S(1)}, bf16[128,896]{1,0:T(8,128)(2,1)S(1)}, u32[]{:S(2)}, u32[]{:S(2)}) collective-permute-start(bf16[128,896]{1,0:T(8,128)(2,1)S(1)} %collective-permute-done.24.refs_0_), channel_id=1, source_target_pairs={{0,2},{1,3},{2,0},{3,1},{4,6},{5,7},{6,4},{7,5},{8,10},{9,11},{10,... | collective-permute-start | bytes 688136 | tf_op jit(solution)/shard_map/ppermute | solution.py:639
  134.2 17.6 %collective-permute-start.27 = (bf16[128,896]{1,0:T(8,128)(2,1)S(1)}, bf16[128,896]{1,0:T(8,128)(2,1)S(1)}, u32[]{:S(2)}, u32[]{:S(2)}) collective-permute-start(bf16[128,896]{1,0:T(8,128)(2,1)S(1)} %collective-permute-done.24.refs_0_), channel_id=1, source_target_pairs={{0,3},{1,2},{2,1},{3,0},{4,7},{5,6},{6,5},{7,4},{8,11},{9,10},{10,... | collective-permute-start | bytes 688136 | tf_op jit(solution)/shard_map/ppermute | solution.py:639
  148.3 16.1 %collective-permute-start.30 = (bf16[128,896]{1,0:T(8,128)(2,1)S(1)}, bf16[128,896]{1,0:T(8,128)(2,1)S(1)}, u32[]{:S(2)}, u32[]{:S(2)}) collective-permute-start(bf16[128,896]{1,0:T(8,128)(2,1)S(1)} %collective-permute-done.29.refs_0_), channel_id=1, source_target_pairs={{0,1},{1,0},{2,3},{3,2},{4,5},{5,4},{6,7},{7,6},{8,9},{9,8},{10,11... | collective-permute-start | bytes 688136 | tf_op jit(solution)/shard_map/ppermute | solution.py:639
  149.3 15.1 %collective-permute-start.31 = (bf16[128,896]{1,0:T(8,128)(2,1)S(1)}, bf16[128,896]{1,0:T(8,128)(2,1)S(1)}, u32[]{:S(2)}, u32[]{:S(2)}) collective-permute-start(bf16[128,896]{1,0:T(8,128)(2,1)S(1)} %collective-permute-done.29.refs_0_), channel_id=1, source_target_pairs={{0,2},{1,3},{2,0},{3,1},{4,6},{5,7},{6,4},{7,5},{8,10},{9,11},{10,... | collective-permute-start | bytes 688136 | tf_op jit(solution)/shard_map/ppermute | solution.py:639
  150.3 14.0 %collective-permute-start.32 = (bf16[128,896]{1,0:T(8,128)(2,1)S(1)}, bf16[128,896]{1,0:T(8,128)(2,1)S(1)}, u32[]{:S(2)}, u32[]{:S(2)}) collective-permute-start(bf16[128,896]{1,0:T(8,128)(2,1)S(1)} %collective-permute-done.29.refs_0_), channel_id=1, source_target_pairs={{0,3},{1,2},{2,1},{3,0},{4,7},{5,6},{6,5},{7,4},{8,11},{9,10},{10,... | collective-permute-start | bytes 688136 | tf_op jit(solution)/shard_map/ppermute | solution.py:639
  178.1 10.9 %all-to-all-start = ((f32[16,3,128]{2,1,0:T(4,128)}), f32[16,3,128]{2,1,0:T(4,128)S(1)}, u32[]{:S(2)}, u32[]{:S(2)}) async-start(f32[16,3,128]{2,1,0:T(4,128)} %gather_fusion), calls=%async_computation | async-start | bytes 65536 | tf_op jit(solution)/shard_map/all_to_all | solution.py:771
  (8 other events, 117.7 us)
